TPU v7x, 32 devices: a whole 2x2x4 slice. The times are simulated.
32 devices in a mesh: row: 8 (over y, x, core), col: 4 (over z).
Axes of the slice: x: 2, y: 2, z: 4, core: 2. Of those that a mesh axis runs over, the one named last changes fastest.
Arguments:
- rotation: bfloat16 [8192, 8192], P('row', 'col'), may hold values from -0.0625 to 0.0625
- gradient: bfloat16 [8192, 8192], P('row', 'col'), may hold values from -0.0625 to 0.0625
Outputs:
- updated: float32 [8192, 2048], P('row', 'col')
- column_norms: float32 [2048], P('col')
All inputs are finite; a program needn't handle non-finite values.
Results may differ from a plain program's by a relative error of at most 0.01.
Values may be sent and summed in bfloat16 or wider, within the bound.
No kernel may reach another device: no remote copies, remote signals or barrier semaphores. Data moves between devices by JAX's collectives and lax.ppermute only.
A program may use at most 128 MiB of HBM per device.

v0:
```python
import jax
import jax.numpy as jnp
from jax import lax
from jax.sharding import PartitionSpec as P


STRIDE = 4
SHARES = (4, 4, 4, 4)
GATHERED = (0, 1, 2, 3)
PLAN = (
    "B0", "C0", "B1", "D0", "C1", "E0", "B2", "D1", "F0", "C2", "B3", "D2",
    "E1", "C3", "E2", "G0", "F1", "D3", "A4", "F2", "E3", "B4", "G1", "F3",
    "C4", "A5", "D4", "G2", "B5", "E4", "A6", "C5", "G3", "B6", "D5", "F4",
    "A7", "C6", "E5", "B7", "D6", "F5", "C7", "E6", "D7", "F6", "E7", "F7",
)


f32, bf16 = jnp.float32, jnp.bfloat16


def mm(a, b):
    return lax.dot_general(a, b, (((1,), (0,)), ((), ())), preferred_element_type=f32)


def mm_t(a, b):
    return lax.dot_general(a, b, (((1,), (1,)), ((), ())), preferred_element_type=f32)


def tie(arrays, token):
    if token is None:
        return list(arrays)
    return list(lax.optimization_barrier((*arrays, token))[:-1])


def solution(mesh):
    rows, cols = mesh.shape["row"], mesh.shape["col"]
    bits = (rows // 2).bit_length() - 1
    blocks = 1 << bits
    sigmas = (tuple(range(bits)), tuple(range(bits))[::-1])
    orders = [
        sorted(range(blocks), key=lambda j, s=s: tuple(j >> b & 1 for b in s)) for s in sigmas
    ]

    def swap(v, mask):
        return lax.ppermute(v, "row", [(i, i ^ mask) for i in range(rows)])

    def turn(v, step):
        return lax.ppermute(v, "col", [(i, (i + step) % cols) for i in range(cols)])

    def on_device(rotation, gradient):
        me_row, me_col = lax.axis_index("row"), lax.axis_index("col")
        core, place = me_row % 2, me_row // 2
        local_rows, local_k = rotation.shape
        block = local_k // blocks
        count = local_k // STRIDE
        half = count // 2
        unit = half // sum(SHARES)
        edges = [0]
        for s in SHARES:
            edges.append(edges[-1] + s * unit)
        n = len(SHARES)

        t = lax.broadcasted_iota(jnp.int32, (count, local_k), 0)
        k = lax.broadcasted_iota(jnp.int32, (count, local_k), 1)
        pick = (k == STRIDE * ((t + half * core) % count)).astype(bf16)
        base_own = mm_t(pick, rotation).astype(bf16)
        base_other = base_own[half:]
        base = jnp.concatenate([base_own[:half], swap(base_other, 1)], axis=1)
        bases = [base[a:b] for a, b in zip(edges, edges[1:])]

        def spread(w, order):
            parts = [
                lax.dynamic_slice_in_dim(w, (j ^ place) * block, block, axis=1) for j in order
            ]
            own = lax.optimization_barrier(jnp.concatenate(parts, axis=1))
            return jnp.concatenate([own, swap(own, 1)], axis=0)

        x_late, g_late = tie([rotation, gradient], base_other)
        weights = [spread(w, o) for w, o in zip((x_late, g_late), orders)]
        turned = list(lax.optimization_barrier(tuple(w.T for w in weights)))
        token_start = turned[1]
        mid_k = local_k // 2

        state = [dict() for _ in range(2 * n)]
        token = [token_start]

        def step(arrays):
            return tie(arrays, token[0])

        def start_panel(k, own):
            state[k]["ups"], state[k]["downs"] = [own], [own]
            state[k]["ups"].append(turn(own, 1))
            if cols > 2:
                state[k]["downs"].append(turn(own, -1))

        def forward_panel(k):
            s = state[k]
            ups, downs = s["ups"], s["downs"]
            while len(ups) + len(downs) < cols + 1:
                if len(ups) <= len(downs):
                    ups.append(turn(ups[-1], 1))
                else:
                    downs.append(turn(downs[-1], -1))

        def multiply(k):
            s = state[k]
            if k in GATHERED:
                panel = lax.all_gather(bases[k], "col", axis=0, tiled=True)
                (panel,) = step([panel])
            else:
                ups, downs = s["ups"], s["downs"]
                near = step(ups + downs[1:])
                ups, downs = near[: len(ups)], [None] + near[len(ups) :]

                def pick_piece(z, j):
                    d = (z - j) % cols
                    return ups[d] if d < len(ups) else downs[cols - d]

                panel = jnp.concatenate(
                    [
                        lax.select_n(me_col, *[pick_piece(z, j) for z in range(cols)])
                        for j in range(cols)
                    ],
                    axis=0,
                )
            panel = lax.optimization_barrier(panel)
            sent = [mm(panel, w[:, mid_k:]).astype(bf16) for w in weights]
            s["recv"] = [swap(v, 2 << sg[0]) for v, sg in zip(sent, sigmas)]
            kept = [
                mm(tie([panel], v)[0], w[:, :mid_k]).astype(bf16)
                for w, v in zip(weights, sent)
            ]
            s["terms"] = [[v] for v in lax.optimization_barrier(tuple(kept))]
            token[0] = kept[1]

        def add(k, t):
            s = state[k]
            depth = len(s["terms"][0])
            flat = step(s["recv"] + s["terms"][0] + s["terms"][1])
            groups = [[flat[0], *flat[2 : 2 + depth]], [flat[1], *flat[2 + depth :]]]
            low = half_k = groups[0][0].shape[1]
            if t + 1 < bits:
                low = half_k // 2

            def total(group, a, b):
                return sum(v[:, a:b].astype(f32) for v in group[1:]) + group[0][:, a:b].astype(f32)

            if t + 1 < bits:
                sent = [total(group, low, half_k).astype(bf16) for group in groups]
                s["recv"] = [swap(v, 2 << sg[t + 1]) for v, sg in zip(sent, sigmas)]
                s["terms"] = groups
                token[0] = sent[1]
            else:
                whole = [total(group, 0, low).astype(bf16) for group in groups]
                s["part"] = [[w, swap(w, 2 << sg[t])] for w, sg in zip(whole, sigmas)]
                token[0] = whole[1]

        def widen(k, t):
            s = state[k]
            got = step([p[1] for p in s["part"]])
            whole = [jnp.concatenate([p[0], g], axis=1) for p, g in zip(s["part"], got)]
            s["part"] = [[w, swap(w, 2 << sg[t])] for w, sg in zip(whole, sigmas)]
            token[0] = whole[1]

        def finish(k):
            s = state[k]
            got = step([p[1] for p in s["part"]])
            full = []
            for i in (0, 1):
                pieces = [
                    p[:, a : a + block]
                    for p in (s["part"][i][0], got[i])
                    for a in range(0, p.shape[1], block)
                ]
                by_block = dict(zip(orders[i], pieces))
                full.append(jnp.concatenate([by_block[j] for j in orders[1 - i]], axis=1))
            full = lax.optimization_barrier(tuple(full))
            term = (mm(full[0], turned[1]) - mm(full[1], turned[0])).astype(bf16)
            token[0] = term
            s["term"] = lax.psum_scatter(term, "col", scatter_dimension=0, tiled=True)

        def middle(k):
            (term,) = step([state[k]["term"]])
            wide = bases[k].astype(f32)
            mid = (wide + (wide + 0.25 * term.astype(f32))).astype(bf16)
            token[0] = mid
            start_panel(k + n, mid)

        last = 2 * n

        def early(k):
            start_panel(k, bases[k])

        def sums(k):
            for t in range(bits - 1):
                add(k, t)

        def widens(k):
            for t in range(bits - 2, -1, -1):
                widen(k, t)

        steps = {
            "A": forward_panel,
            "B": multiply,
            "C": sums,
            "D": lambda k: add(k, bits - 1),
            "E": widens,
            "F": finish,
            "G": middle,
        }
        for k in range(n):
            if k not in GATHERED:
                early(k)
        for name in PLAN:
            steps[name[0]](int(name[1:]))

        terms = [state[k]["term"] for k in range(n, last)]
        ups = [b.astype(f32) + 0.125 * t.astype(f32) for b, t in zip(bases, terms)]
        squares = jnp.concatenate([jnp.sum(u * u, axis=1) for u in ups])
        mine = jnp.concatenate([u[:, :local_rows] for u in ups], axis=0)
        fetched = swap(jnp.concatenate([t[:, local_rows:] for t in terms], axis=0), 1)
        other = base_other.astype(f32) + 0.125 * fetched.astype(f32)
        low = jnp.where(core == 0, mine, other)
        high = jnp.where(core == 0, other, mine)
        updated = jnp.concatenate([low, high], axis=0).T
        squares = squares + sum(swap(squares, 2 * j) for j in range(1, blocks))
        pair = swap(squares, 1)
        norms = jnp.where(
            core == 0, jnp.concatenate([squares, pair]), jnp.concatenate([pair, squares])
        )
        return (updated, jnp.sqrt(norms))

    return jax.shard_map(
        on_device,
        mesh=mesh,
        in_specs=(P("row", "col"), P("row", "col")),
        out_specs=(P("row", "col"), P("col")),
        check_vma=False,
    )
```

profile of v0, /device:TPU:0, one launch (start us, length us, event | category | flops | bytes accessed | tf_op | source)
XLA Modules:
  0.0 528.2 jit_solution(17591812279701239898)
XLA Ops:
  7.3 4.6 fusion.19
  28.6 8.4 %fusion = bf16[2048,2048]{0,1:T(8,128)(2,1)} fusion(bf16[1024,2048]{1,0:T(8,128)(2,1)} %collective-permute-done.2, bf16[1024,2048]{1,0:T(8,128)(2,1)} %pad_maximum_fusion.3), kind=kLoop, calls=%fused_computation.10 | loop fusion | flops 16777216 | bytes 16777216 | tf_op jit(solution)/shard_map/transpose | solution.py:80
  37.0 8.4 %fusion.1 = bf16[2048,2048]{0,1:T(8,128)(2,1)} fusion(bf16[1024,2048]{1,0:T(8,128)(2,1)} %collective-permute-done.1, bf16[1024,2048]{1,0:T(8,128)(2,1)} %pad_maximum_fusion.2), kind=kLoop, calls=%fused_computation.11 | loop fusion | flops 16777216 | bytes 16777216 | tf_op jit(solution)/shard_map/transpose | solution.py:80
  46.8 4.2 fusion.3
  54.4 4.4 fusion.5
  66.7 7.3 %collective-permute-done.3 = bf16[256,1024]{1,0:T(8,128)(2,1)S(1)} collective-permute-done((bf16[256,1024]{1,0:T(8,128)(2,1)S(1)}, bf16[256,1024]{1,0:T(8,128)(2,1)S(1)}, u32[]{:S(2)}, u32[]{:S(2)}) %collective-permute-start.3) | collective-permute-done | bytes 524320 | tf_op jit(solution)/shard_map/ppermute | solution.py:45
  75.8 3.9 convolution_convert_fusion.25
  88.0 12.0 %collective-permute-done.6 = bf16[256,512]{1,0:T(8,128)(2,1)S(1)} collective-permute-done((bf16[256,512]{1,0:T(8,128)(2,1)S(1)}, bf16[256,512]{1,0:T(8,128)(2,1)S(1)}, u32[]{:S(2)}, u32[]{:S(2)}) %collective-permute-start.6) | collective-permute-done | bytes 262176 | tf_op jit(solution)/shard_map/ppermute | solution.py:45
  106.2 4.3 collective-permute-done.8
  114.9 4.7 convolution_convert_fusion.23
  130.7 7.7 %collective-permute-done.11 = bf16[256,1024]{1,0:T(8,128)(2,1)S(1)} collective-permute-done((bf16[256,1024]{1,0:T(8,128)(2,1)S(1)}, bf16[256,1024]{1,0:T(8,128)(2,1)S(1)}, u32[]{:S(2)}, u32[]{:S(2)}) %collective-permute-start.11) | collective-permute-done | bytes 524320 | tf_op jit(solution)/shard_map/ppermute | solution.py:45
  143.8 3.3 fusion.7
  148.9 4.7 convolution_convert_fusion.19
  159.0 3.8 convolution_convert_fusion.18
  164.1 12.1 %collective-permute-done.17 = bf16[256,512]{1,0:T(8,128)(2,1)S(1)} collective-permute-done((bf16[256,512]{1,0:T(8,128)(2,1)S(1)}, bf16[256,512]{1,0:T(8,128)(2,1)S(1)}, u32[]{:S(2)}, u32[]{:S(2)}) %collective-permute-start.17) | collective-permute-done | bytes 262176 | tf_op jit(solution)/shard_map/ppermute | solution.py:45
  193.8 5.7 %collective-permute-done.30 = bf16[256,1024]{1,0:T(8,128)(2,1)} collective-permute-done((bf16[256,1024]{1,0:T(8,128)(2,1)}, bf16[256,1024]{1,0:T(8,128)(2,1)}, u32[]{:S(2)}, u32[]{:S(2)}) %collective-permute-start.30) | collective-permute-done | bytes 524320 | tf_op jit(solution)/shard_map/ppermute | solution.py:45
  204.0 5.9 %fusion.50 = f32[256,2048]{1,0:T(8,128)S(1)} fusion(bf16[256,2048]{1,0:T(8,128)(2,1)S(1)} %pad_maximum_fusion.7, bf16[2048,2048]{0,1:T(8,128)(2,1)} %fusion.1), kind=kOutput, calls=%fused_computation.225 | convolution fusion | flops 2147483648 | bytes 11534336 | tf_op jit(solution)/shard_map/dot_general | solution.py:22
  209.9 3.3 fusion.8
  213.3 3.2 collective-permute-start.27
  221.5 5.9 %fusion.51 = f32[256,2048]{1,0:T(8,128)S(1)} fusion(bf16[256,2048]{1,0:T(8,128)(2,1)S(1)} %pad_maximum_fusion.9, bf16[2048,2048]{0,1:T(8,128)(2,1)} %fusion.1), kind=kOutput, calls=%fused_computation.226 | convolution fusion | flops 2147483648 | bytes 11534336 | tf_op jit(solution)/shard_map/dot_general | solution.py:22
  229.9 3.4 fusion.9
  233.6 4.2 collective-permute-done.32
  256.8 5.9 %fusion.52 = f32[256,2048]{1,0:T(8,128)S(1)} fusion(bf16[256,2048]{1,0:T(8,128)(2,1)S(1)} %pad_maximum_fusion.12, bf16[2048,2048]{0,1:T(8,128)(2,1)} %fusion.1), kind=kOutput, calls=%fused_computation.227 | convolution fusion | flops 2147483648 | bytes 11534336 | tf_op jit(solution)/shard_map/dot_general | solution.py:22
  262.8 3.3 fusion.10
  269.6 3.8 collective-permute-start.46
  277.2 3.5 collective-permute-done.44
  283.1 2.7 collective-permute-start.55
  288.3 6.4 %collective-permute-done.45 = bf16[64,2048]{1,0:T(8,128)(2,1)S(1)} collective-permute-done((bf16[64,2048]{1,0:T(8,128)(2,1)S(1)}, bf16[64,2048]{1,0:T(8,128)(2,1)S(1)}, u32[]{:S(2)}, u32[]{:S(2)}) %collective-permute-start.45) | collective-permute-done | bytes 262176 | tf_op jit(solution)/shard_map/ppermute | solution.py:48
  307.2 3.8 collective-permute-done.50
  311.0 3.4 collective-permute-done.49
  342.9 3.3 fusion.11
  346.3 4.2 convolution_convert_fusion.4
  350.6 3.8 collective-permute-start.66
  358.3 5.9 %collective-permute-done.66 = bf16[64,2048]{1,0:T(8,128)(2,1)S(1)} collective-permute-done((bf16[64,2048]{1,0:T(8,128)(2,1)S(1)}, bf16[64,2048]{1,0:T(8,128)(2,1)S(1)}, u32[]{:S(2)}, u32[]{:S(2)}) %collective-permute-start.66) | collective-permute-done | bytes 262176 | tf_op jit(solution)/shard_map/ppermute | solution.py:48
  364.2 8.5 %collective-permute-done.65 = bf16[64,2048]{1,0:T(8,128)(2,1)S(1)} collective-permute-done((bf16[64,2048]{1,0:T(8,128)(2,1)}, bf16[64,2048]{1,0:T(8,128)(2,1)S(1)}, u32[]{:S(2)}, u32[]{:S(2)}) %collective-permute-start.65) | collective-permute-done | bytes 262176 | tf_op jit(solution)/shard_map/ppermute | solution.py:48
  386.9 6.3 %collective-permute-done.62 = bf16[256,512]{1,0:T(8,128)(2,1)S(1)} collective-permute-done((bf16[256,512]{1,0:T(8,128)(2,1)S(1)}, bf16[256,512]{1,0:T(8,128)(2,1)S(1)}, u32[]{:S(2)}, u32[]{:S(2)}) %collective-permute-start.62) | collective-permute-done | bytes 262176 | tf_op jit(solution)/shard_map/ppermute | solution.py:45
  402.4 3.3 fusion.12
  405.7 3.7 collective-permute-done.69
  411.3 3.7 collective-permute-done.68
  427.1 5.8 %collective-permute-done.72 = bf16[256,1024]{1,0:T(8,128)(2,1)} collective-permute-done((bf16[256,1024]{1,0:T(8,128)(2,1)}, bf16[256,1024]{1,0:T(8,128)(2,1)}, u32[]{:S(2)}, u32[]{:S(2)}) %collective-permute-start.72) | collective-permute-done | bytes 524320 | tf_op jit(solution)/shard_map/ppermute | solution.py:45
  435.7 5.9 %fusion.55 = f32[256,2048]{1,0:T(8,128)S(1)} fusion(bf16[256,2048]{1,0:T(8,128)(2,1)S(1)} %pad_maximum_fusion.21, bf16[2048,2048]{0,1:T(8,128)(2,1)} %fusion.1), kind=kOutput, calls=%fused_computation.230 | convolution fusion | flops 2147483648 | bytes 11534336 | tf_op jit(solution)/shard_map/dot_general | solution.py:22
  441.7 3.4 fusion.13
  450.3 4.0 collective-permute-done.78
  454.4 3.4 collective-permute-done.77
  459.3 5.9 %fusion.56 = f32[256,2048]{1,0:T(8,128)S(1)} fusion(bf16[256,2048]{1,0:T(8,128)(2,1)S(1)} %pad_maximum_fusion.23, bf16[2048,2048]{0,1:T(8,128)(2,1)} %fusion.1), kind=kOutput, calls=%fused_computation.231 | convolution fusion | flops 2147483648 | bytes 11534336 | tf_op jit(solution)/shard_map/dot_general | solution.py:22
  465.2 3.3 fusion.14
  472.0 5.1 reduce-scatter.21.cloned.1.call-done
  479.9 25.7 %reduce-scatter.23.cloned.1.call-done = bf16[64,2048]{1,0:T(8,128)(2,1)} async-done(((bf16[256,2048]{1,0:T(8,128)(2,1)}), bf16[64,2048]{1,0:T(8,128)(2,1)}) %reduce-scatter.23.cloned.1.call-update) | async-done | bytes 262160 | tf_op jit(solution)/shard_map/reduce_scatter | solution.py:180
  (538 shorter events, 248.1 us)
Async XLA Ops:
  7.2 39.6 %all-gather.5.cloned.1.call-start = ((), (), s32[]{:S(2)}) async-start(), calls=%async_computation.8 | async-start | bytes 1310720 | tf_op jit(solution)/shard_map/all_gather | solution.py:108
  16.1 59.7 %all-gather.7.cloned.1.call-start = ((), (), s32[]{:S(2)}) async-start(), calls=%async_computation.9 | async-start | bytes 1310720 | tf_op jit(solution)/shard_map/all_gather | solution.py:108
  25.5 89.3 %all-gather.9.cloned.1.call-start = ((), (), s32[]{:S(2)}) async-start(), calls=%async_computation.10 | async-start | bytes 1310720 | tf_op jit(solution)/shard_map/all_gather | solution.py:108
  26.3 122.6 %all-gather.11.cloned.1.call-start = ((), (), s32[]{:S(2)}) async-start(), calls=%async_computation.12 | async-start | bytes 1310720 | tf_op jit(solution)/shard_map/all_gather | solution.py:108
  26.9 165.9 %reduce-scatter.9.cloned.1.call-start = ((), (), s32[]{:S(2)}) async-start(), calls=%async_computation.11 | async-start | bytes 1310720 | tf_op jit(solution)/shard_map/reduce_scatter | solution.py:180
  81.1 23.7 %collective-permute-start.9 = (bf16[256,1024]{1,0:T(8,128)(2,1)S(1)}, bf16[256,1024]{1,0:T(8,128)(2,1)S(1)}, u32[]{:S(2)}, u32[]{:S(2)}) collective-permute-start(bf16[256,1024]{1,0:T(8,128)(2,1)S(1)} %convolution_convert_fusion.25), channel_id=1, source_target_pairs={{0,8},{4,12},{8,0},{12,4},{16,24},{20,28},{24,16},{28,20},{1,9},{5... | collective-permute-start | bytes 1572872 | tf_op jit(solution)/shard_map/ppermute | solution.py:45
  82.6 17.3 %collective-permute-start.6 = (bf16[256,512]{1,0:T(8,128)(2,1)S(1)}, bf16[256,512]{1,0:T(8,128)(2,1)S(1)}, u32[]{:S(2)}, u32[]{:S(2)}) collective-permute-start(bf16[256,512]{1,0:T(8,128)(2,1)S(1)} %add_convert_fusion.30), channel_id=1, source_target_pairs={{0,8},{4,12},{8,0},{12,4},{16,24},{20,28},{24,16},{28,20},{1,9},{5... | collective-permute-start | bytes 786440 | tf_op jit(solution)/shard_map/ppermute | solution.py:45
  83.2 21.6 %collective-permute-start.10 = (bf16[256,1024]{1,0:T(8,128)(2,1)S(1)}, bf16[256,1024]{1,0:T(8,128)(2,1)S(1)}, u32[]{:S(2)}, u32[]{:S(2)}) collective-permute-start(bf16[256,1024]{1,0:T(8,128)(2,1)S(1)} %convolution_convert_fusion.27), channel_id=1, source_target_pairs={{0,16},{4,20},{8,24},{12,28},{16,0},{20,4},{24,8},{28,12},{1,17},{... | collective-permute-start | bytes 1572872 | tf_op jit(solution)/shard_map/ppermute | solution.py:45
  104.9 21.7 %collective-permute-start.13 = (bf16[256,512]{1,0:T(8,128)(2,1)S(1)}, bf16[256,512]{1,0:T(8,128)(2,1)}, u32[]{:S(2)}, u32[]{:S(2)}) collective-permute-start(bf16[256,512]{1,0:T(8,128)(2,1)S(1)} %add_convert_fusion.26), channel_id=1, source_target_pairs={{0,16},{4,20},{8,24},{12,28},{16,0},{20,4},{24,8},{28,12},{1,17},{... | collective-permute-start | bytes 786440 | tf_op jit(solution)/shard_map/ppermute | solution.py:45
  105.6 22.4 %collective-permute-start.14 = (bf16[256,512]{1,0:T(8,128)(2,1)S(1)}, bf16[256,512]{1,0:T(8,128)(2,1)S(1)}, u32[]{:S(2)}, u32[]{:S(2)}) collective-permute-start(bf16[256,512]{1,0:T(8,128)(2,1)S(1)} %add_convert_fusion.27), channel_id=1, source_target_pairs={{0,8},{4,12},{8,0},{12,4},{16,24},{20,28},{24,16},{28,20},{1,9},{5... | collective-permute-start | bytes 786440 | tf_op jit(solution)/shard_map/ppermute | solution.py:45
  113.4 25.7 %collective-permute-start.12 = (bf16[256,1024]{1,0:T(8,128)(2,1)}, bf16[256,1024]{1,0:T(8,128)(2,1)}, u32[]{:S(2)}, u32[]{:S(2)}) collective-permute-start(bf16[256,1024]{1,0:T(8,128)(2,1)} %pad_maximum_fusion.26), channel_id=1, source_target_pairs={{0,16},{4,20},{8,24},{12,28},{16,0},{20,4},{24,8},{28,12},{1,17},{... | collective-permute-start | bytes 1572872 | tf_op jit(solution)/shard_map/ppermute | solution.py:45
  121.6 25.5 %collective-permute-start.16 = (bf16[256,1024]{1,0:T(8,128)(2,1)}, bf16[256,1024]{1,0:T(8,128)(2,1)S(1)}, u32[]{:S(2)}, u32[]{:S(2)}) collective-permute-start(bf16[256,1024]{1,0:T(8,128)(2,1)} %convolution_convert_fusion.23), channel_id=1, source_target_pairs={{0,16},{4,20},{8,24},{12,28},{16,0},{20,4},{24,8},{28,12},{1,17},{... | collective-permute-start | bytes 1572872 | tf_op jit(solution)/shard_map/ppermute | solution.py:45
  126.6 21.4 %collective-permute-start.15 = (bf16[256,1024]{1,0:T(8,128)(2,1)}, bf16[256,1024]{1,0:T(8,128)(2,1)}, u32[]{:S(2)}, u32[]{:S(2)}) collective-permute-start(bf16[256,1024]{1,0:T(8,128)(2,1)} %convolution_convert_fusion.21), channel_id=1, source_target_pairs={{0,8},{4,12},{8,0},{12,4},{16,24},{20,28},{24,16},{28,20},{1,9},{5... | collective-permute-start | bytes 1572872 | tf_op jit(solution)/shard_map/ppermute | solution.py:45
  129.1 51.0 %collective-permute-start.23 = (bf16[256,512]{1,0:T(8,128)(2,1)S(1)}, bf16[256,512]{1,0:T(8,128)(2,1)S(1)}, u32[]{:S(2)}, u32[]{:S(2)}) collective-permute-start(bf16[256,512]{1,0:T(8,128)(2,1)S(1)} %add_convert_fusion.20), channel_id=1, source_target_pairs={{0,16},{4,20},{8,24},{12,28},{16,0},{20,4},{24,8},{28,12},{1,17},{... | collective-permute-start | bytes 786440 | tf_op jit(solution)/shard_map/ppermute | solution.py:45
  138.4 42.6 %collective-permute-start.24 = (bf16[256,512]{1,0:T(8,128)(2,1)S(1)}, bf16[256,512]{1,0:T(8,128)(2,1)S(1)}, u32[]{:S(2)}, u32[]{:S(2)}) collective-permute-start(bf16[256,512]{1,0:T(8,128)(2,1)S(1)} %add_convert_fusion.25), channel_id=1, source_target_pairs={{0,8},{4,12},{8,0},{12,4},{16,24},{20,28},{24,16},{28,20},{1,9},{5... | collective-permute-start | bytes 786440 | tf_op jit(solution)/shard_map/ppermute | solution.py:45
  148.1 29.1 %collective-permute-start.18 = (bf16[256,512]{1,0:T(8,128)(2,1)S(1)}, bf16[256,512]{1,0:T(8,128)(2,1)S(1)}, u32[]{:S(2)}, u32[]{:S(2)}) collective-permute-start(bf16[256,512]{1,0:T(8,128)(2,1)S(1)} %add_convert_fusion.23), channel_id=1, source_target_pairs={{0,8},{4,12},{8,0},{12,4},{16,24},{20,28},{24,16},{28,20},{1,9},{5... | collective-permute-start | bytes 786440 | tf_op jit(solution)/shard_map/ppermute | solution.py:45
  155.7 28.2 %collective-permute-start.22 = (bf16[256,1024]{1,0:T(8,128)(2,1)}, bf16[256,1024]{1,0:T(8,128)(2,1)}, u32[]{:S(2)}, u32[]{:S(2)}) collective-permute-start(bf16[256,1024]{1,0:T(8,128)(2,1)} %convolution_convert_fusion.19), channel_id=1, source_target_pairs={{0,16},{4,20},{8,24},{12,28},{16,0},{20,4},{24,8},{28,12},{1,17},{... | collective-permute-start | bytes 1572872 | tf_op jit(solution)/shard_map/ppermute | solution.py:45
  157.0 96.3 %reduce-scatter.11.cloned.1.call-start = ((), (), s32[]{:S(2)}) async-start(), calls=%async_computation.13 | async-start | bytes 1310720 | tf_op jit(solution)/shard_map/reduce_scatter | solution.py:180
  158.3 17.9 %collective-permute-start.17 = (bf16[256,512]{1,0:T(8,128)(2,1)S(1)}, bf16[256,512]{1,0:T(8,128)(2,1)S(1)}, u32[]{:S(2)}, u32[]{:S(2)}) collective-permute-start(bf16[256,512]{1,0:T(8,128)(2,1)S(1)} %add_convert_fusion.24), channel_id=1, source_target_pairs={{0,16},{4,20},{8,24},{12,28},{16,0},{20,4},{24,8},{28,12},{1,17},{... | collective-permute-start | bytes 786440 | tf_op jit(solution)/shard_map/ppermute | solution.py:45
  181.9 17.7 %collective-permute-start.30 = (bf16[256,1024]{1,0:T(8,128)(2,1)}, bf16[256,1024]{1,0:T(8,128)(2,1)}, u32[]{:S(2)}, u32[]{:S(2)}) collective-permute-start(bf16[256,1024]{1,0:T(8,128)(2,1)} %pad_maximum_fusion.29), channel_id=1, source_target_pairs={{0,8},{4,12},{8,0},{12,4},{16,24},{20,28},{24,16},{28,20},{1,9},{5... | collective-permute-start | bytes 1572872 | tf_op jit(solution)/shard_map/ppermute | solution.py:45
  187.3 26.0 %collective-permute-start.29 = (bf16[256,512]{1,0:T(8,128)(2,1)}, bf16[256,512]{1,0:T(8,128)(2,1)}, u32[]{:S(2)}, u32[]{:S(2)}) collective-permute-start(bf16[256,512]{1,0:T(8,128)(2,1)} %add_convert_fusion.19), channel_id=1, source_target_pairs={{0,8},{4,12},{8,0},{12,4},{16,24},{20,28},{24,16},{28,20},{1,9},{5... | collective-permute-start | bytes 786440 | tf_op jit(solution)/shard_map/ppermute | solution.py:45
  189.0 27.5 %collective-permute-start.28 = (bf16[256,512]{1,0:T(8,128)(2,1)}, bf16[256,512]{1,0:T(8,128)(2,1)}, u32[]{:S(2)}, u32[]{:S(2)}) collective-permute-start(bf16[256,512]{1,0:T(8,128)(2,1)} %add_convert_fusion.18), channel_id=1, source_target_pairs={{0,16},{4,20},{8,24},{12,28},{16,0},{20,4},{24,8},{28,12},{1,17},{... | collective-permute-start | bytes 786440 | tf_op jit(solution)/shard_map/ppermute | solution.py:45
  192.4 26.5 %collective-permute-start.35 = (bf16[256,1024]{1,0:T(8,128)(2,1)}, bf16[256,1024]{1,0:T(8,128)(2,1)}, u32[]{:S(2)}, u32[]{:S(2)}) collective-permute-start(bf16[256,1024]{1,0:T(8,128)(2,1)} %pad_maximum_fusion.28), channel_id=1, source_target_pairs={{0,16},{4,20},{8,24},{12,28},{16,0},{20,4},{24,8},{28,12},{1,17},{... | collective-permute-start | bytes 1572872 | tf_op jit(solution)/shard_map/ppermute | solution.py:45
  199.6 19.3 %collective-permute-start.34 = (bf16[256,1024]{1,0:T(8,128)(2,1)}, bf16[256,1024]{1,0:T(8,128)(2,1)}, u32[]{:S(2)}, u32[]{:S(2)}) collective-permute-start(bf16[256,1024]{1,0:T(8,128)(2,1)} %pad_maximum_fusion.30), channel_id=1, source_target_pairs={{0,8},{4,12},{8,0},{12,4},{16,24},{20,28},{24,16},{28,20},{1,9},{5... | collective-permute-start | bytes 1572872 | tf_op jit(solution)/shard_map/ppermute | solution.py:45
  200.5 29.4 %collective-permute-start.25 = (bf16[64,2048]{1,0:T(8,128)(2,1)S(1)}, bf16[64,2048]{1,0:T(8,128)(2,1)S(1)}, u32[]{:S(2)}, u32[]{:S(2)}) collective-permute-start(bf16[64,2048]{1,0:T(8,128)(2,1)S(1)} %fusion.22), channel_id=1, source_target_pairs={{0,1},{1,2},{2,3},{3,0},{4,5},{5,6},{6,7},{7,4},{8,9},{9,10},{10,1... | collective-permute-start | bytes 786440 | tf_op jit(solution)/shard_map/ppermute | solution.py:48
  213.3 63.9 %reduce-scatter.13.cloned.1.call-start = ((), (), s32[]{:S(2)}) async-start(), calls=%async_computation.14 | async-start | bytes 1310720 | tf_op jit(solution)/shard_map/reduce_scatter | solution.py:180
  213.3 28.7 %collective-permute-start.27 = (bf16[64,2048]{1,0:T(8,128)(2,1)S(1)}, bf16[64,2048]{1,0:T(8,128)(2,1)S(1)}, u32[]{:S(2)}, u32[]{:S(2)}) collective-permute-start(bf16[64,2048]{1,0:T(8,128)(2,1)S(1)} %fusion.22), channel_id=1, source_target_pairs={{0,3},{1,0},{2,1},{3,2},{4,7},{5,4},{6,5},{7,6},{8,11},{9,8},{10,9... | collective-permute-start | bytes 786440 | tf_op jit(solution)/shard_map/ppermute | solution.py:48
  233.3 86.3 %reduce-scatter.15.cloned.1.call-start = ((), (), s32[]{:S(2)}) async-start(), calls=%async_computation.15 | async-start | bytes 1310720 | tf_op jit(solution)/shard_map/reduce_scatter | solution.py:180
  248.0 18.1 %collective-permute-start.36 = (bf16[256,1024]{1,0:T(8,128)(2,1)}, bf16[256,1024]{1,0:T(8,128)(2,1)S(1)}, u32[]{:S(2)}, u32[]{:S(2)}) collective-permute-start(bf16[256,1024]{1,0:T(8,128)(2,1)} %convolution_convert_fusion.15), channel_id=1, source_target_pairs={{0,8},{4,12},{8,0},{12,4},{16,24},{20,28},{24,16},{28,20},{1,9},{5... | collective-permute-start | bytes 1572872 | tf_op jit(solution)/shard_map/ppermute | solution.py:45
  269.6 17.4 %collective-permute-start.46 = (bf16[64,2048]{1,0:T(8,128)(2,1)S(1)}, bf16[64,2048]{1,0:T(8,128)(2,1)}, u32[]{:S(2)}, u32[]{:S(2)}) collective-permute-start(bf16[64,2048]{1,0:T(8,128)(2,1)S(1)} %fusion.23), channel_id=1, source_target_pairs={{0,3},{1,0},{2,1},{3,2},{4,7},{5,4},{6,5},{7,6},{8,11},{9,8},{10,9... | collective-permute-start | bytes 786440 | tf_op jit(solution)/shard_map/ppermute | solution.py:48
  273.5 195.2 %reduce-scatter.17.cloned.1.call-start = ((), (), s32[]{:S(2)}) async-start(), calls=%async_computation.16 | async-start | bytes 1310720 | tf_op jit(solution)/shard_map/reduce_scatter | solution.py:180
  276.1 25.2 %collective-permute-start.43 = (bf16[256,512]{1,0:T(8,128)(2,1)S(1)}, bf16[256,512]{1,0:T(8,128)(2,1)S(1)}, u32[]{:S(2)}, u32[]{:S(2)}) collective-permute-start(bf16[256,512]{1,0:T(8,128)(2,1)S(1)} %add_convert_fusion.12), channel_id=1, source_target_pairs={{0,8},{4,12},{8,0},{12,4},{16,24},{20,28},{24,16},{28,20},{1,9},{5... | collective-permute-start | bytes 786440 | tf_op jit(solution)/shard_map/ppermute | solution.py:45
  281.8 24.4 %collective-permute-start.53 = (bf16[64,2048]{1,0:T(8,128)(2,1)S(1)}, bf16[64,2048]{1,0:T(8,128)(2,1)S(1)}, u32[]{:S(2)}, u32[]{:S(2)}) collective-permute-start(bf16[64,2048]{1,0:T(8,128)(2,1)S(1)} %fusion.24), channel_id=1, source_target_pairs={{0,1},{1,2},{2,3},{3,0},{4,5},{5,6},{6,7},{7,4},{8,9},{9,10},{10,1... | collective-permute-start | bytes 786440 | tf_op jit(solution)/shard_map/ppermute | solution.py:48
  283.1 37.7 %collective-permute-start.55 = (bf16[64,2048]{1,0:T(8,128)(2,1)S(1)}, bf16[64,2048]{1,0:T(8,128)(2,1)}, u32[]{:S(2)}, u32[]{:S(2)}) collective-permute-start(bf16[64,2048]{1,0:T(8,128)(2,1)S(1)} %fusion.24), channel_id=1, source_target_pairs={{0,3},{1,0},{2,1},{3,2},{4,7},{5,4},{6,5},{7,6},{8,11},{9,8},{10,9... | collective-permute-start | bytes 786440 | tf_op jit(solution)/shard_map/ppermute | solution.py:48
  302.2 33.1 %collective-permute-start.47 = (bf16[256,1024]{1,0:T(8,128)(2,1)}, bf16[256,1024]{1,0:T(8,128)(2,1)}, u32[]{:S(2)}, u32[]{:S(2)}) collective-permute-start(bf16[256,1024]{1,0:T(8,128)(2,1)} %pad_maximum_fusion.33), channel_id=1, source_target_pairs={{0,8},{4,12},{8,0},{12,4},{16,24},{20,28},{24,16},{28,20},{1,9},{5... | collective-permute-start | bytes 1572872 | tf_op jit(solution)/shard_map/ppermute | solution.py:45
  306.2 29.1 %collective-permute-start.48 = (bf16[256,1024]{1,0:T(8,128)(2,1)}, bf16[256,1024]{1,0:T(8,128)(2,1)}, u32[]{:S(2)}, u32[]{:S(2)}) collective-permute-start(bf16[256,1024]{1,0:T(8,128)(2,1)} %pad_maximum_fusion.34), channel_id=1, source_target_pairs={{0,16},{4,20},{8,24},{12,28},{16,0},{20,4},{24,8},{28,12},{1,17},{... | collective-permute-start | bytes 1572872 | tf_op jit(solution)/shard_map/ppermute | solution.py:45
  325.9 29.0 %collective-permute-start.59 = (bf16[256,1024]{1,0:T(8,128)(2,1)}, bf16[256,1024]{1,0:T(8,128)(2,1)}, u32[]{:S(2)}, u32[]{:S(2)}) collective-permute-start(bf16[256,1024]{1,0:T(8,128)(2,1)} %convolution_convert_fusion.7), channel_id=1, source_target_pairs={{0,16},{4,20},{8,24},{12,28},{16,0},{20,4},{24,8},{28,12},{1,17},{... | collective-permute-start | bytes 1572872 | tf_op jit(solution)/shard_map/ppermute | solution.py:45
  330.3 20.3 %collective-permute-start.64 = (bf16[64,2048]{1,0:T(8,128)(2,1)S(1)}, bf16[64,2048]{1,0:T(8,128)(2,1)}, u32[]{:S(2)}, u32[]{:S(2)}) collective-permute-start(bf16[64,2048]{1,0:T(8,128)(2,1)S(1)} %fusion.25), channel_id=1, source_target_pairs={{0,1},{1,2},{2,3},{3,0},{4,5},{5,6},{6,7},{7,4},{8,9},{9,10},{10,1... | collective-permute-start | bytes 786440 | tf_op jit(solution)/shard_map/ppermute | solution.py:48
  331.6 25.9 %collective-permute-start.57 = (bf16[256,512]{1,0:T(8,128)(2,1)S(1)}, bf16[256,512]{1,0:T(8,128)(2,1)S(1)}, u32[]{:S(2)}, u32[]{:S(2)}) collective-permute-start(bf16[256,512]{1,0:T(8,128)(2,1)S(1)} %add_convert_fusion.9), channel_id=1, source_target_pairs={{0,8},{4,12},{8,0},{12,4},{16,24},{20,28},{24,16},{28,20},{1,9},{5... | collective-permute-start | bytes 786440 | tf_op jit(solution)/shard_map/ppermute | solution.py:45
  350.5 119.4 %reduce-scatter.19.cloned.1.call-start = ((), (), s32[]{:S(2)}) async-start(), calls=%async_computation.17 | async-start | bytes 1310720 | tf_op jit(solution)/shard_map/reduce_scatter | solution.py:180
  354.4 18.3 %collective-permute-start.65 = (bf16[64,2048]{1,0:T(8,128)(2,1)}, bf16[64,2048]{1,0:T(8,128)(2,1)S(1)}, u32[]{:S(2)}, u32[]{:S(2)}) collective-permute-start(bf16[64,2048]{1,0:T(8,128)(2,1)} %collective-permute-done.64), channel_id=1, source_target_pairs={{0,1},{1,2},{2,3},{3,0},{4,5},{5,6},{6,7},{7,4},{8,9},{9,10},{10,1... | collective-permute-start | bytes 786440 | tf_op jit(solution)/shard_map/ppermute | solution.py:48
  356.0 38.5 %collective-permute-start.63 = (bf16[256,512]{1,0:T(8,128)(2,1)S(1)}, bf16[256,512]{1,0:T(8,128)(2,1)S(1)}, u32[]{:S(2)}, u32[]{:S(2)}) collective-permute-start(bf16[256,512]{1,0:T(8,128)(2,1)S(1)} %add_convert_fusion.7), channel_id=1, source_target_pairs={{0,8},{4,12},{8,0},{12,4},{16,24},{20,28},{24,16},{28,20},{1,9},{5... | collective-permute-start | bytes 786440 | tf_op jit(solution)/shard_map/ppermute | solution.py:45
  357.6 41.2 %collective-permute-start.61 = (bf16[256,1024]{1,0:T(8,128)(2,1)S(1)}, bf16[256,1024]{1,0:T(8,128)(2,1)S(1)}, u32[]{:S(2)}, u32[]{:S(2)}) collective-permute-start(bf16[256,1024]{1,0:T(8,128)(2,1)S(1)} %pad_maximum_fusion.36), channel_id=1, source_target_pairs={{0,16},{4,20},{8,24},{12,28},{16,0},{20,4},{24,8},{28,12},{1,17},{... | collective-permute-start | bytes 1572872 | tf_op jit(solution)/shard_map/ppermute | solution.py:45
  378.3 27.5 %collective-permute-start.70 = (bf16[256,1024]{1,0:T(8,128)(2,1)}, bf16[256,1024]{1,0:T(8,128)(2,1)}, u32[]{:S(2)}, u32[]{:S(2)}) collective-permute-start(bf16[256,1024]{1,0:T(8,128)(2,1)} %convolution_convert_fusion.3), channel_id=1, source_target_pairs={{0,16},{4,20},{8,24},{12,28},{16,0},{20,4},{24,8},{28,12},{1,17},{... | collective-permute-start | bytes 1572872 | tf_op jit(solution)/shard_map/ppermute | solution.py:45
  421.2 55.9 %reduce-scatter.21.cloned.1.call-start = ((), (), s32[]{:S(2)}) async-start(), calls=%async_computation.18 | async-start | bytes 1310720 | tf_op jit(solution)/shard_map/reduce_scatter | solution.py:180
  424.5 20.6 %collective-permute-start.76 = (bf16[256,512]{1,0:T(8,128)(2,1)S(1)}, bf16[256,512]{1,0:T(8,128)(2,1)S(1)}, u32[]{:S(2)}, u32[]{:S(2)}) collective-permute-start(bf16[256,512]{1,0:T(8,128)(2,1)S(1)} %add_convert_fusion.1), channel_id=1, source_target_pairs={{0,8},{4,12},{8,0},{12,4},{16,24},{20,28},{24,16},{28,20},{1,9},{5... | collective-permute-start | bytes 786440 | tf_op jit(solution)/shard_map/ppermute | solution.py:45
  426.5 18.6 %collective-permute-start.75 = (bf16[256,512]{1,0:T(8,128)(2,1)S(1)}, bf16[256,512]{1,0:T(8,128)(2,1)S(1)}, u32[]{:S(2)}, u32[]{:S(2)}) collective-permute-start(bf16[256,512]{1,0:T(8,128)(2,1)S(1)} %add_convert_fusion), channel_id=1, source_target_pairs={{0,16},{4,20},{8,24},{12,28},{16,0},{20,4},{24,8},{28,12},{1,17},{... | collective-permute-start | bytes 786440 | tf_op jit(solution)/shard_map/ppermute | solution.py:45
  450.3 55.3 %reduce-scatter.23.cloned.1.call-start = ((), (), s32[]{:S(2)}) async-start(), calls=%async_computation.19 | async-start | bytes 1310720 | tf_op jit(solution)/shard_map/reduce_scatter | solution.py:180
  (148 other events, 1394.1 us)
Sparse Core Ops, SparseCore 0:
  16.2 30.5 all-gather.4
  48.4 27.3 all-gather.6
  77.3 27.3 all-gather.8
  106.2 27.3 all-gather.10
  157.2 27.1 reduce-scatter.8
  213.4 30.1 reduce-scatter.10
  245.8 29.7 reduce-scatter.12
  278.5 41.0 reduce-scatter.14
  350.7 31.2 reduce-scatter.16
  421.3 27.5 reduce-scatter.18
  451.3 25.7 reduce-scatter.20
  479.8 25.7 reduce-scatter.22
where the time goes:
time: 535 us; the launch traced here: 528 us
  waiting for transfers between devices  172 us (32%)
  matrix products  134 us (25%)
  starting transfers between devices  92.2 us (17%)
  other arithmetic  85.8 us (16%)
  local copies, waits for them, and re-layouts  27.6 us (5%)
  between operations  16.2 us (3%)
    dot_general x48, matrix products, mm(): lax.dot_general(a, b, (((1,), (0,)), ((), ())), preferred_element_type=f32)  130 us
    ppermute x72, waiting for transfers between devices, swap(): return lax.ppermute(v, 'row', [(i, i ^ mask) for i in range(rows)])  109 us
    ppermute x72, starting transfers between devices, swap(): return lax.ppermute(v, 'row', [(i, i ^ mask) for i in range(rows)])  74.7 us
    reduce_scatter x8, waiting for transfers between devices, finish(): s['term'] = lax.psum_scatter(term, 'col', scatter_dimension=0, tiled=True)  32.6 us
    ppermute x12, waiting for transfers between devices, turn(): return lax.ppermute(v, 'col', [(i, (i + step) % cols) for i in range(cols)])  25.8 us
    transpose x2, other arithmetic, on_device(): turned = list(lax.optimization_barrier(tuple((w.T for w in weights))))  16.8 us
    ppermute x12, starting transfers between devices, turn(): return lax.ppermute(v, 'col', [(i, (i + step) % cols) for i in range(cols)])  16.7 us
    slice x16, local copies, waits for them, and re-layouts, finish(): p[:, a:a + block]  13.8 us
  transfers between devices with their start and end apart: 96, of which 42 were waited for; matrix products, arithmetic and copies ran while one was open for 44% of the time, Pallas kernels for 0%

commit v1 on v0

--- a/solution.py
+++ b/solution.py
@@ -8,10 +8,10 @@
 SHARES = (4, 4, 4, 4)
 GATHERED = (0, 1, 2, 3)
 PLAN = (
-    "B0", "C0", "B1", "D0", "C1", "E0", "B2", "D1", "F0", "C2", "B3", "D2",
-    "E1", "C3", "E2", "G0", "F1", "D3", "A4", "F2", "E3", "B4", "G1", "F3",
-    "C4", "A5", "D4", "G2", "B5", "E4", "A6", "C5", "G3", "B6", "D5", "F4",
-    "A7", "C6", "E5", "B7", "D6", "F5", "C7", "E6", "D7", "F6", "E7", "F7",
+    "B0", "C0", "B1", "E0", "C1", "B2", "F0", "E1", "B3", "C2", "F1", "C3",
+    "G0", "E2", "E3", "A4", "F2", "G1", "B4", "F3", "A5", "C4", "G2", "B5",
+    "E4", "A6", "C5", "G3", "B6", "F4", "A7", "E5", "C6", "B7", "F5", "E6",
+    "C7", "F6", "E7", "F7",
 )
 
 
@@ -37,9 +37,6 @@
     bits = (rows // 2).bit_length() - 1
     blocks = 1 << bits
     sigmas = (tuple(range(bits)), tuple(range(bits))[::-1])
-    orders = [
-        sorted(range(blocks), key=lambda j, s=s: tuple(j >> b & 1 for b in s)) for s in sigmas
-    ]
 
     def swap(v, mask):
         return lax.ppermute(v, "row", [(i, i ^ mask) for i in range(rows)])
@@ -51,7 +48,6 @@
         me_row, me_col = lax.axis_index("row"), lax.axis_index("col")
         core, place = me_row % 2, me_row // 2
         local_rows, local_k = rotation.shape
-        block = local_k // blocks
         count = local_k // STRIDE
         half = count // 2
         unit = half // sum(SHARES)
@@ -68,18 +64,19 @@
         base = jnp.concatenate([base_own[:half], swap(base_other, 1)], axis=1)
         bases = [base[a:b] for a, b in zip(edges, edges[1:])]
 
-        def spread(w, order):
+        def spread(w, bit):
             parts = [
-                lax.dynamic_slice_in_dim(w, (j ^ place) * block, block, axis=1) for j in order
+                lax.dynamic_slice_in_dim(w, (j ^ bit) * mid_k, mid_k, axis=1) for j in (0, 1)
             ]
             own = lax.optimization_barrier(jnp.concatenate(parts, axis=1))
             return jnp.concatenate([own, swap(own, 1)], axis=0)
 
+        mid_k = local_k // 2
+        ends = [place >> sg[0] & 1 for sg in sigmas]
         x_late, g_late = tie([rotation, gradient], base_other)
-        weights = [spread(w, o) for w, o in zip((x_late, g_late), orders)]
+        weights = [spread(w, o) for w, o in zip((x_late, g_late), ends)]
         turned = list(lax.optimization_barrier(tuple(w.T for w in weights)))
         token_start = turned[1]
-        mid_k = local_k // 2
 
         state = [dict() for _ in range(2 * n)]
         token = [token_start]
@@ -130,50 +127,27 @@
                 mm(tie([panel], v)[0], w[:, :mid_k]).astype(bf16)
                 for w, v in zip(weights, sent)
             ]
-            s["terms"] = [[v] for v in lax.optimization_barrier(tuple(kept))]
+            s["kept"] = list(lax.optimization_barrier(tuple(kept)))
             token[0] = kept[1]
 
-        def add(k, t):
-            s = state[k]
-            depth = len(s["terms"][0])
-            flat = step(s["recv"] + s["terms"][0] + s["terms"][1])
-            groups = [[flat[0], *flat[2 : 2 + depth]], [flat[1], *flat[2 + depth :]]]
-            low = half_k = groups[0][0].shape[1]
-            if t + 1 < bits:
-                low = half_k // 2
-
-            def total(group, a, b):
-                return sum(v[:, a:b].astype(f32) for v in group[1:]) + group[0][:, a:b].astype(f32)
-
-            if t + 1 < bits:
-                sent = [total(group, low, half_k).astype(bf16) for group in groups]
-                s["recv"] = [swap(v, 2 << sg[t + 1]) for v, sg in zip(sent, sigmas)]
-                s["terms"] = groups
-                token[0] = sent[1]
-            else:
-                whole = [total(group, 0, low).astype(bf16) for group in groups]
-                s["part"] = [[w, swap(w, 2 << sg[t])] for w, sg in zip(whole, sigmas)]
-                token[0] = whole[1]
-
-        def widen(k, t):
-            s = state[k]
-            got = step([p[1] for p in s["part"]])
-            whole = [jnp.concatenate([p[0], g], axis=1) for p, g in zip(s["part"], got)]
-            s["part"] = [[w, swap(w, 2 << sg[t])] for w, sg in zip(whole, sigmas)]
-            token[0] = whole[1]
+        def exchange(k, t):
+            s = state[k]
+            flat = step(s["recv"] + s["kept"])
+            sums = [(flat[i].astype(f32) + flat[2 + i].astype(f32)).astype(bf16) for i in (0, 1)]
+            s["recv"] = [swap(v, 2 << sg[t]) for v, sg in zip(sums, sigmas)]
+            s["kept"] = sums
+            token[0] = sums[1]
 
         def finish(k):
             s = state[k]
-            got = step([p[1] for p in s["part"]])
-            full = []
-            for i in (0, 1):
-                pieces = [
-                    p[:, a : a + block]
-                    for p in (s["part"][i][0], got[i])
-                    for a in range(0, p.shape[1], block)
-                ]
-                by_block = dict(zip(orders[i], pieces))
-                full.append(jnp.concatenate([by_block[j] for j in orders[1 - i]], axis=1))
+            flat = step(s["recv"] + s["kept"])
+            same = ends[0] == ends[1]
+            full = [
+                jnp.concatenate(
+                    [jnp.where(same, own, got), jnp.where(same, got, own)], axis=1
+                )
+                for got, own in zip(flat[:2], flat[2:])
+            ]
             full = lax.optimization_barrier(tuple(full))
             term = (mm(full[0], turned[1]) - mm(full[1], turned[0])).astype(bf16)
             token[0] = term
@@ -191,20 +165,15 @@
         def early(k):
             start_panel(k, bases[k])
 
-        def sums(k):
-            for t in range(bits - 1):
-                add(k, t)
-
-        def widens(k):
-            for t in range(bits - 2, -1, -1):
-                widen(k, t)
+        def middles(k):
+            for t in range(1, bits):
+                exchange(k, t)
 
         steps = {
             "A": forward_panel,
             "B": multiply,
-            "C": sums,
-            "D": lambda k: add(k, bits - 1),
-            "E": widens,
+            "C": middles,
+            "E": lambda k: exchange(k, 0),
             "F": finish,
             "G": middle,
         }

time: 535 us -> 551 us (1.030)
  waiting for transfers between devices: 172 us -> 197 us
  local copies, waits for them, and re-layouts: 27.6 us -> 19.1 us
    reduce_scatter x8, waiting for transfers between devices: 32.6 us -> 61.4 us  [finish(): s['term'] = lax.psum_scatter(term, 'col', scatter_dimension=0, tiled=True)]
    slice x16 -> x0, local copies, waits for them, and re-layouts: 13.8 us -> none  [finish(): p[:, a:a + block]]
    concatenate x32 -> x16, other arithmetic: 12.9 us -> 1.28 us  [finish(): jnp.concatenate([jnp.where(same, own, got), jnp.where(same, got, own)], a...]
    ppermute x72 -> x56, starting transfers between devices: 74.7 us -> 65.7 us  [swap(): return lax.ppermute(v, 'row', [(i, i ^ mask) for i in range(rows)])]
    select_n x0 -> x16, other arithmetic: none -> 8.12 us  [finish(): jnp.where(same, own, got)]
    ppermute x12, waiting for transfers between devices: 25.8 us -> 18.8 us  [turn(): return lax.ppermute(v, 'col', [(i, (i + step) % cols) for i in range(cols)])]
    ppermute x72 -> x56, waiting for transfers between devices: 109 us -> 115 us  [swap(): return lax.ppermute(v, 'row', [(i, i ^ mask) for i in range(rows)])]
  transfers between devices with their start and end apart: 96 -> 80, of which waited for: 42 -> 31; matrix products, arithmetic and copies ran while one was open for 44% -> 41% of each run, Pallas kernels for 0% -> 0%
where the time goes in v1:
time: 551 us; the launch traced here: 543 us
  waiting for transfers between devices  197 us (36%)
  matrix products  136 us (25%)
  starting transfers between devices  88 us (16%)
  other arithmetic  86.2 us (16%)
  local copies, waits for them, and re-layouts  19.1 us (3%)
  between operations  16.5 us (3%)
    dot_general x48, matrix products, mm(): lax.dot_general(a, b, (((1,), (0,)), ((), ())), preferred_element_type=f32)  131 us
    ppermute x56, waiting for transfers between devices, swap(): return lax.ppermute(v, 'row', [(i, i ^ mask) for i in range(rows)])  115 us
    ppermute x56, starting transfers between devices, swap(): return lax.ppermute(v, 'row', [(i, i ^ mask) for i in range(rows)])  65.7 us
    reduce_scatter x8, waiting for transfers between devices, finish(): s['term'] = lax.psum_scatter(term, 'col', scatter_dimension=0, tiled=True)  61.4 us
    convert_element_type x32, other arithmetic, exchange(): (flat[i].astype(f32) + flat[2 + i].astype(f32)).astype(bf16)  26.9 us
    ppermute x12, starting transfers between devices, turn(): return lax.ppermute(v, 'col', [(i, (i + step) % cols) for i in range(cols)])  21.3 us
    ppermute x12, waiting for transfers between devices, turn(): return lax.ppermute(v, 'col', [(i, (i + step) % cols) for i in range(cols)])  18.8 us
    transpose x2, other arithmetic, on_device(): turned = list(lax.optimization_barrier(tuple((w.T for w in weights))))  16.9 us
  transfers between devices with their start and end apart: 80, of which 31 were waited for; matrix products, arithmetic and copies ran while one was open for 41% of the time, Pallas kernels for 0%

profile of v1, /device:TPU:0, one launch (start us, length us, event | category | flops | bytes accessed | tf_op | source)
XLA Modules:
  0.0 543.2 jit_solution(12406365254155906212)
XLA Ops:
  7.3 4.6 fusion.19
  28.7 8.5 %fusion = bf16[2048,2048]{0,1:T(8,128)(2,1)} fusion(bf16[1024,2048]{1,0:T(8,128)(2,1)} %collective-permute-done.2, bf16[1024,2048]{1,0:T(8,128)(2,1)} %pad_maximum_fusion.3), kind=kLoop, calls=%fused_computation.10 | loop fusion | flops 16777216 | bytes 16777216 | tf_op jit(solution)/shard_map/transpose | solution.py:78
  37.2 8.4 %fusion.1 = bf16[2048,2048]{0,1:T(8,128)(2,1)} fusion(bf16[1024,2048]{1,0:T(8,128)(2,1)} %collective-permute-done.1, bf16[1024,2048]{1,0:T(8,128)(2,1)} %pad_maximum_fusion.2), kind=kLoop, calls=%fused_computation.11 | loop fusion | flops 16777216 | bytes 16777216 | tf_op jit(solution)/shard_map/transpose | solution.py:78
  46.8 4.2 fusion.3
  54.8 4.4 fusion.5
  67.0 7.3 %collective-permute-done.3 = bf16[256,1024]{1,0:T(8,128)(2,1)S(1)} collective-permute-done((bf16[256,1024]{1,0:T(8,128)(2,1)S(1)}, bf16[256,1024]{1,0:T(8,128)(2,1)S(1)}, u32[]{:S(2)}, u32[]{:S(2)}) %collective-permute-start.3) | collective-permute-done | bytes 524320 | tf_op jit(solution)/shard_map/ppermute | solution.py:42
  76.2 3.9 convolution_convert_fusion.27
  88.4 17.2 %collective-permute-done.5 = bf16[256,1024]{1,0:T(8,128)(2,1)S(1)} collective-permute-done((bf16[256,1024]{1,0:T(8,128)(2,1)S(1)}, bf16[256,1024]{1,0:T(8,128)(2,1)S(1)}, u32[]{:S(2)}, u32[]{:S(2)}) %collective-permute-start.5) | collective-permute-done | bytes 524320 | tf_op jit(solution)/shard_map/ppermute | solution.py:42
  106.6 4.7 convolution_convert_fusion.17
  124.5 23.8 %collective-permute-done.7 = bf16[256,1024]{1,0:T(8,128)(2,1)S(1)} collective-permute-done((bf16[256,1024]{1,0:T(8,128)(2,1)S(1)}, bf16[256,1024]{1,0:T(8,128)(2,1)S(1)}, u32[]{:S(2)}, u32[]{:S(2)}) %collective-permute-start.7) | collective-permute-done | bytes 524320 | tf_op jit(solution)/shard_map/ppermute | solution.py:42
  153.8 3.3 fusion.7
  157.1 2.9 collective-permute-done.11
  163.1 4.7 convolution_convert_fusion.20
  172.1 4.7 convolution_convert_fusion.18
  182.8 10.0 %collective-permute-done.15 = bf16[256,1024]{1,0:T(8,128)(2,1)S(1)} collective-permute-done((bf16[256,1024]{1,0:T(8,128)(2,1)S(1)}, bf16[256,1024]{1,0:T(8,128)(2,1)S(1)}, u32[]{:S(2)}, u32[]{:S(2)}) %collective-permute-start.15) | collective-permute-done | bytes 524320 | tf_op jit(solution)/shard_map/ppermute | solution.py:42
  200.1 3.3 fusion.8
  209.1 3.7 collective-permute-start.21
  216.3 3.1 collective-permute-done.27
  224.4 6.2 %collective-permute-done.24 = bf16[256,1024]{1,0:T(8,128)(2,1)S(1)} collective-permute-done((bf16[256,1024]{1,0:T(8,128)(2,1)S(1)}, bf16[256,1024]{1,0:T(8,128)(2,1)S(1)}, u32[]{:S(2)}, u32[]{:S(2)}) %collective-permute-start.24) | collective-permute-done | bytes 524320 | tf_op jit(solution)/shard_map/ppermute | solution.py:42
  232.7 5.9 %fusion.35 = f32[256,2048]{1,0:T(8,128)S(1)} fusion(bf16[256,2048]{1,0:T(8,128)(2,1)S(1)} %pad_maximum_fusion.9, bf16[2048,2048]{0,1:T(8,128)(2,1)} %fusion.1), kind=kOutput, calls=%fused_computation.222 | convolution fusion | flops 2147483648 | bytes 11534336 | tf_op jit(solution)/shard_map/dot_general | solution.py:22
  238.6 3.3 fusion.9
  251.5 3.3 collective-permute-start.36
  254.8 4.5 convolution_convert_fusion.12
  265.3 3.3 fusion.10
  268.6 3.5 convolution_convert_fusion.13
  277.7 8.6 %reduce-scatter.13.cloned.1.call-done = bf16[64,2048]{1,0:T(8,128)(2,1)} async-done(((bf16[256,2048]{1,0:T(8,128)(2,1)}), bf16[64,2048]{1,0:T(8,128)(2,1)}) %reduce-scatter.13.cloned.1.call-update) | async-done | bytes 262160 | tf_op jit(solution)/shard_map/reduce_scatter | solution.py:154
  294.5 3.4 collective-permute-start.42
  299.9 3.3 collective-permute-start.41
  308.0 6.6 %collective-permute-done.39 = bf16[64,2048]{1,0:T(8,128)(2,1)S(1)} collective-permute-done((bf16[64,2048]{1,0:T(8,128)(2,1)S(1)}, bf16[64,2048]{1,0:T(8,128)(2,1)S(1)}, u32[]{:S(2)}, u32[]{:S(2)}) %collective-permute-start.39) | collective-permute-done | bytes 262176 | tf_op jit(solution)/shard_map/ppermute | solution.py:45
  314.9 4.5 collective-permute-start.40
  320.4 12.5 %reduce-scatter.15.cloned.1.call-done = bf16[64,2048]{1,0:T(8,128)(2,1)} async-done(((bf16[256,2048]{1,0:T(8,128)(2,1)}), bf16[64,2048]{1,0:T(8,128)(2,1)}) %reduce-scatter.15.cloned.1.call-update) | async-done | bytes 262160 | tf_op jit(solution)/shard_map/reduce_scatter | solution.py:154
  352.7 3.3 fusion.11
  356.0 4.6 convolution_convert_fusion.4
  360.7 3.8 collective-permute-start.50
  369.6 3.8 collective-permute-start.54
  373.4 2.8 collective-permute-done.50
  376.3 8.9 %collective-permute-done.49 = bf16[64,2048]{1,0:T(8,128)(2,1)S(1)} collective-permute-done((bf16[64,2048]{1,0:T(8,128)(2,1)}, bf16[64,2048]{1,0:T(8,128)(2,1)S(1)}, u32[]{:S(2)}, u32[]{:S(2)}) %collective-permute-start.49) | collective-permute-done | bytes 262176 | tf_op jit(solution)/shard_map/ppermute | solution.py:45
  397.3 14.2 %collective-permute-done.46 = bf16[256,1024]{1,0:T(8,128)(2,1)S(1)} collective-permute-done((bf16[256,1024]{1,0:T(8,128)(2,1)S(1)}, bf16[256,1024]{1,0:T(8,128)(2,1)S(1)}, u32[]{:S(2)}, u32[]{:S(2)}) %collective-permute-start.46) | collective-permute-done | bytes 524320 | tf_op jit(solution)/shard_map/ppermute | solution.py:42
  416.3 3.4 fusion.12
  430.6 6.3 %collective-permute-done.55 = bf16[256,1024]{1,0:T(8,128)(2,1)} collective-permute-done((bf16[256,1024]{1,0:T(8,128)(2,1)S(1)}, bf16[256,1024]{1,0:T(8,128)(2,1)}, u32[]{:S(2)}, u32[]{:S(2)}) %collective-permute-start.55) | collective-permute-done | bytes 524320 | tf_op jit(solution)/shard_map/ppermute | solution.py:42
  436.9 3.1 collective-permute-done.56
  442.6 5.9 %fusion.39 = f32[256,2048]{1,0:T(8,128)S(1)} fusion(bf16[256,2048]{1,0:T(8,128)(2,1)S(1)} %pad_maximum_fusion.21, bf16[2048,2048]{0,1:T(8,128)(2,1)} %fusion.1), kind=kOutput, calls=%fused_computation.226 | convolution fusion | flops 2147483648 | bytes 11534336 | tf_op jit(solution)/shard_map/dot_general | solution.py:22
  448.5 3.3 fusion.13
  455.2 7.2 %collective-permute-done.62 = bf16[256,1024]{1,0:T(8,128)(2,1)S(1)} collective-permute-done((bf16[256,1024]{1,0:T(8,128)(2,1)S(1)}, bf16[256,1024]{1,0:T(8,128)(2,1)S(1)}, u32[]{:S(2)}, u32[]{:S(2)}) %collective-permute-start.62) | collective-permute-done | bytes 524320 | tf_op jit(solution)/shard_map/ppermute | solution.py:42
  464.5 5.9 %fusion.40 = f32[256,2048]{1,0:T(8,128)S(1)} fusion(bf16[256,2048]{1,0:T(8,128)(2,1)S(1)} %pad_maximum_fusion.23, bf16[2048,2048]{0,1:T(8,128)(2,1)} %fusion.1), kind=kOutput, calls=%fused_computation.227 | convolution fusion | flops 2147483648 | bytes 11534336 | tf_op jit(solution)/shard_map/dot_general | solution.py:22
  470.4 3.3 fusion.14
  477.2 14.6 %reduce-scatter.21.cloned.1.call-done = bf16[64,2048]{1,0:T(8,128)(2,1)} async-done(((bf16[256,2048]{1,0:T(8,128)(2,1)}), bf16[64,2048]{1,0:T(8,128)(2,1)}) %reduce-scatter.21.cloned.1.call-update) | async-done | bytes 262160 | tf_op jit(solution)/shard_map/reduce_scatter | solution.py:154
  494.7 25.6 %reduce-scatter.23.cloned.1.call-done = bf16[64,2048]{1,0:T(8,128)(2,1)} async-done(((bf16[256,2048]{1,0:T(8,128)(2,1)}), bf16[64,2048]{1,0:T(8,128)(2,1)}) %reduce-scatter.23.cloned.1.call-update) | async-done | bytes 262160 | tf_op jit(solution)/shard_map/reduce_scatter | solution.py:154
  (444 shorter events, 214.7 us)
Async XLA Ops:
  7.2 39.7 %all-gather.5.cloned.1.call-start = ((), (), s32[]{:S(2)}) async-start(), calls=%async_computation.8 | async-start | bytes 1310720 | tf_op jit(solution)/shard_map/all_gather | solution.py:105
  16.1 60.1 %all-gather.7.cloned.1.call-start = ((), (), s32[]{:S(2)}) async-start(), calls=%async_computation.9 | async-start | bytes 1310720 | tf_op jit(solution)/shard_map/all_gather | solution.py:105
  26.9 79.7 %all-gather.9.cloned.1.call-start = ((), (), s32[]{:S(2)}) async-start(), calls=%async_computation.10 | async-start | bytes 1310720 | tf_op jit(solution)/shard_map/all_gather | solution.py:105
  27.7 135.4 %all-gather.11.cloned.1.call-start = ((), (), s32[]{:S(2)}) async-start(), calls=%async_computation.12 | async-start | bytes 1310720 | tf_op jit(solution)/shard_map/all_gather | solution.py:105
  28.2 179.6 %reduce-scatter.9.cloned.1.call-start = ((), (), s32[]{:S(2)}) async-start(), calls=%async_computation.11 | async-start | bytes 1310720 | tf_op jit(solution)/shard_map/reduce_scatter | solution.py:154
  74.6 31.0 %collective-permute-start.6 = (bf16[256,1024]{1,0:T(8,128)(2,1)S(1)}, bf16[256,1024]{1,0:T(8,128)(2,1)S(1)}, u32[]{:S(2)}, u32[]{:S(2)}) collective-permute-start(bf16[256,1024]{1,0:T(8,128)(2,1)S(1)} %add_convert_fusion.30), channel_id=1, source_target_pairs={{0,8},{4,12},{8,0},{12,4},{16,24},{20,28},{24,16},{28,20},{1,9},{5... | collective-permute-start | bytes 1572872 | tf_op jit(solution)/shard_map/ppermute | solution.py:42
  81.5 24.3 %collective-permute-start.10 = (bf16[256,1024]{1,0:T(8,128)(2,1)S(1)}, bf16[256,1024]{1,0:T(8,128)(2,1)S(1)}, u32[]{:S(2)}, u32[]{:S(2)}) collective-permute-start(bf16[256,1024]{1,0:T(8,128)(2,1)S(1)} %convolution_convert_fusion.27), channel_id=1, source_target_pairs={{0,16},{4,20},{8,24},{12,28},{16,0},{20,4},{24,8},{28,12},{1,17},{... | collective-permute-start | bytes 1572872 | tf_op jit(solution)/shard_map/ppermute | solution.py:42
  82.8 22.7 %collective-permute-start.5 = (bf16[256,1024]{1,0:T(8,128)(2,1)S(1)}, bf16[256,1024]{1,0:T(8,128)(2,1)S(1)}, u32[]{:S(2)}, u32[]{:S(2)}) collective-permute-start(bf16[256,1024]{1,0:T(8,128)(2,1)S(1)} %add_convert_fusion.31), channel_id=1, source_target_pairs={{0,16},{4,20},{8,24},{12,28},{16,0},{20,4},{24,8},{28,12},{1,17},{... | collective-permute-start | bytes 1572872 | tf_op jit(solution)/shard_map/ppermute | solution.py:42
  85.1 21.3 %collective-permute-start.9 = (bf16[256,1024]{1,0:T(8,128)(2,1)S(1)}, bf16[256,1024]{1,0:T(8,128)(2,1)}, u32[]{:S(2)}, u32[]{:S(2)}) collective-permute-start(bf16[256,1024]{1,0:T(8,128)(2,1)S(1)} %convolution_convert_fusion.25), channel_id=1, source_target_pairs={{0,8},{4,12},{8,0},{12,4},{16,24},{20,28},{24,16},{28,20},{1,9},{5... | collective-permute-start | bytes 1572872 | tf_op jit(solution)/shard_map/ppermute | solution.py:42
  113.5 63.4 %collective-permute-start.17 = (bf16[256,1024]{1,0:T(8,128)(2,1)}, bf16[256,1024]{1,0:T(8,128)(2,1)S(1)}, u32[]{:S(2)}, u32[]{:S(2)}) collective-permute-start(bf16[256,1024]{1,0:T(8,128)(2,1)} %convolution_convert_fusion.17), channel_id=1, source_target_pairs={{0,8},{4,12},{8,0},{12,4},{16,24},{20,28},{24,16},{28,20},{1,9},{5... | collective-permute-start | bytes 1572872 | tf_op jit(solution)/shard_map/ppermute | solution.py:42
  115.0 35.1 %collective-permute-start.8 = (bf16[256,1024]{1,0:T(8,128)(2,1)S(1)}, bf16[256,1024]{1,0:T(8,128)(2,1)S(1)}, u32[]{:S(2)}, u32[]{:S(2)}) collective-permute-start(bf16[256,1024]{1,0:T(8,128)(2,1)S(1)} %add_convert_fusion.28), channel_id=1, source_target_pairs={{0,16},{4,20},{8,24},{12,28},{16,0},{20,4},{24,8},{28,12},{1,17},{... | collective-permute-start | bytes 1572872 | tf_op jit(solution)/shard_map/ppermute | solution.py:42
  116.4 40.7 %collective-permute-start.12 = (bf16[256,1024]{1,0:T(8,128)(2,1)S(1)}, bf16[256,1024]{1,0:T(8,128)(2,1)}, u32[]{:S(2)}, u32[]{:S(2)}) collective-permute-start(bf16[256,1024]{1,0:T(8,128)(2,1)S(1)} %add_convert_fusion.27), channel_id=1, source_target_pairs={{0,8},{4,12},{8,0},{12,4},{16,24},{20,28},{24,16},{28,20},{1,9},{5... | collective-permute-start | bytes 1572872 | tf_op jit(solution)/shard_map/ppermute | solution.py:42
  117.0 59.9 %collective-permute-start.18 = (bf16[256,1024]{1,0:T(8,128)(2,1)}, bf16[256,1024]{1,0:T(8,128)(2,1)S(1)}, u32[]{:S(2)}, u32[]{:S(2)}) collective-permute-start(bf16[256,1024]{1,0:T(8,128)(2,1)} %convolution_convert_fusion.23), channel_id=1, source_target_pairs={{0,16},{4,20},{8,24},{12,28},{16,0},{20,4},{24,8},{28,12},{1,17},{... | collective-permute-start | bytes 1572872 | tf_op jit(solution)/shard_map/ppermute | solution.py:42
  119.1 29.3 %collective-permute-start.7 = (bf16[256,1024]{1,0:T(8,128)(2,1)S(1)}, bf16[256,1024]{1,0:T(8,128)(2,1)S(1)}, u32[]{:S(2)}, u32[]{:S(2)}) collective-permute-start(bf16[256,1024]{1,0:T(8,128)(2,1)S(1)} %add_convert_fusion.29), channel_id=1, source_target_pairs={{0,8},{4,12},{8,0},{12,4},{16,24},{20,28},{24,16},{28,20},{1,9},{5... | collective-permute-start | bytes 1572872 | tf_op jit(solution)/shard_map/ppermute | solution.py:42
  161.2 34.1 %collective-permute-start.16 = (bf16[256,1024]{1,0:T(8,128)(2,1)S(1)}, bf16[256,1024]{1,0:T(8,128)(2,1)}, u32[]{:S(2)}, u32[]{:S(2)}) collective-permute-start(bf16[256,1024]{1,0:T(8,128)(2,1)S(1)} %add_convert_fusion.25), channel_id=1, source_target_pairs={{0,16},{4,20},{8,24},{12,28},{16,0},{20,4},{24,8},{28,12},{1,17},{... | collective-permute-start | bytes 1572872 | tf_op jit(solution)/shard_map/ppermute | solution.py:42
  169.8 33.6 %collective-permute-start.14 = (bf16[256,1024]{1,0:T(8,128)(2,1)}, bf16[256,1024]{1,0:T(8,128)(2,1)}, u32[]{:S(2)}, u32[]{:S(2)}) collective-permute-start(bf16[256,1024]{1,0:T(8,128)(2,1)} %convolution_convert_fusion.20), channel_id=1, source_target_pairs={{0,16},{4,20},{8,24},{12,28},{16,0},{20,4},{24,8},{28,12},{1,17},{... | collective-permute-start | bytes 1572872 | tf_op jit(solution)/shard_map/ppermute | solution.py:42
  170.1 33.3 %collective-permute-start.13 = (bf16[256,1024]{1,0:T(8,128)(2,1)}, bf16[256,1024]{1,0:T(8,128)(2,1)}, u32[]{:S(2)}, u32[]{:S(2)}) collective-permute-start(bf16[256,1024]{1,0:T(8,128)(2,1)} %convolution_convert_fusion.21), channel_id=1, source_target_pairs={{0,8},{4,12},{8,0},{12,4},{16,24},{20,28},{24,16},{28,20},{1,9},{5... | collective-permute-start | bytes 1572872 | tf_op jit(solution)/shard_map/ppermute | solution.py:42
  171.9 70.1 %reduce-scatter.11.cloned.1.call-start = ((), (), s32[]{:S(2)}) async-start(), calls=%async_computation.13 | async-start | bytes 1310720 | tf_op jit(solution)/shard_map/reduce_scatter | solution.py:154
  180.8 28.3 %collective-permute-start.22 = (bf16[256,1024]{1,0:T(8,128)(2,1)S(1)}, bf16[256,1024]{1,0:T(8,128)(2,1)S(1)}, u32[]{:S(2)}, u32[]{:S(2)}) collective-permute-start(bf16[256,1024]{1,0:T(8,128)(2,1)S(1)} %add_convert_fusion.21), channel_id=1, source_target_pairs={{0,16},{4,20},{8,24},{12,28},{16,0},{20,4},{24,8},{28,12},{1,17},{... | collective-permute-start | bytes 1572872 | tf_op jit(solution)/shard_map/ppermute | solution.py:42
  192.8 20.0 %collective-permute-start.23 = (bf16[256,1024]{1,0:T(8,128)(2,1)S(1)}, bf16[256,1024]{1,0:T(8,128)(2,1)}, u32[]{:S(2)}, u32[]{:S(2)}) collective-permute-start(bf16[256,1024]{1,0:T(8,128)(2,1)S(1)} %add_convert_fusion.23), channel_id=1, source_target_pairs={{0,8},{4,12},{8,0},{12,4},{16,24},{20,28},{24,16},{28,20},{1,9},{5... | collective-permute-start | bytes 1572872 | tf_op jit(solution)/shard_map/ppermute | solution.py:42
  207.8 78.5 %reduce-scatter.13.cloned.1.call-start = ((), (), s32[]{:S(2)}) async-start(), calls=%async_computation.14 | async-start | bytes 1310720 | tf_op jit(solution)/shard_map/reduce_scatter | solution.py:154
  209.1 34.1 %collective-permute-start.21 = (bf16[64,2048]{1,0:T(8,128)(2,1)S(1)}, bf16[64,2048]{1,0:T(8,128)(2,1)}, u32[]{:S(2)}, u32[]{:S(2)}) collective-permute-start(bf16[64,2048]{1,0:T(8,128)(2,1)S(1)} %fusion.22), channel_id=1, source_target_pairs={{0,3},{1,0},{2,1},{3,2},{4,7},{5,4},{6,5},{7,6},{8,11},{9,8},{10,9... | collective-permute-start | bytes 786440 | tf_op jit(solution)/shard_map/ppermute | solution.py:45
  222.4 36.9 %collective-permute-start.31 = (bf16[256,1024]{1,0:T(8,128)(2,1)S(1)}, bf16[256,1024]{1,0:T(8,128)(2,1)S(1)}, u32[]{:S(2)}, u32[]{:S(2)}) collective-permute-start(bf16[256,1024]{1,0:T(8,128)(2,1)S(1)} %add_convert_fusion.17), channel_id=1, source_target_pairs={{0,16},{4,20},{8,24},{12,28},{16,0},{20,4},{24,8},{28,12},{1,17},{... | collective-permute-start | bytes 1572872 | tf_op jit(solution)/shard_map/ppermute | solution.py:42
  224.0 37.3 %collective-permute-start.30 = (bf16[256,1024]{1,0:T(8,128)(2,1)S(1)}, bf16[256,1024]{1,0:T(8,128)(2,1)}, u32[]{:S(2)}, u32[]{:S(2)}) collective-permute-start(bf16[256,1024]{1,0:T(8,128)(2,1)S(1)} %add_convert_fusion.16), channel_id=1, source_target_pairs={{0,8},{4,12},{8,0},{12,4},{16,24},{20,28},{24,16},{28,20},{1,9},{5... | collective-permute-start | bytes 1572872 | tf_op jit(solution)/shard_map/ppermute | solution.py:42
  248.9 23.4 %collective-permute-start.29 = (bf16[256,1024]{1,0:T(8,128)(2,1)}, bf16[256,1024]{1,0:T(8,128)(2,1)}, u32[]{:S(2)}, u32[]{:S(2)}) collective-permute-start(bf16[256,1024]{1,0:T(8,128)(2,1)} %convolution_convert_fusion.14), channel_id=1, source_target_pairs={{0,16},{4,20},{8,24},{12,28},{16,0},{20,4},{24,8},{28,12},{1,17},{... | collective-permute-start | bytes 1572872 | tf_op jit(solution)/shard_map/ppermute | solution.py:42
  250.5 82.4 %reduce-scatter.15.cloned.1.call-start = ((), (), s32[]{:S(2)}) async-start(), calls=%async_computation.15 | async-start | bytes 1310720 | tf_op jit(solution)/shard_map/reduce_scatter | solution.py:154
  250.5 21.7 %collective-permute-start.34 = (bf16[64,2048]{1,0:T(8,128)(2,1)S(1)}, bf16[64,2048]{1,0:T(8,128)(2,1)}, u32[]{:S(2)}, u32[]{:S(2)}) collective-permute-start(bf16[64,2048]{1,0:T(8,128)(2,1)S(1)} %fusion.23), channel_id=1, source_target_pairs={{0,1},{1,2},{2,3},{3,0},{4,5},{5,6},{6,7},{7,4},{8,9},{9,10},{10,1... | collective-permute-start | bytes 786440 | tf_op jit(solution)/shard_map/ppermute | solution.py:45
  251.5 36.0 %collective-permute-start.36 = (bf16[64,2048]{1,0:T(8,128)(2,1)S(1)}, bf16[64,2048]{1,0:T(8,128)(2,1)}, u32[]{:S(2)}, u32[]{:S(2)}) collective-permute-start(bf16[64,2048]{1,0:T(8,128)(2,1)S(1)} %fusion.23), channel_id=1, source_target_pairs={{0,3},{1,0},{2,1},{3,2},{4,7},{5,4},{6,5},{7,6},{8,11},{9,8},{10,9... | collective-permute-start | bytes 786440 | tf_op jit(solution)/shard_map/ppermute | solution.py:45
  272.2 201.6 %reduce-scatter.17.cloned.1.call-start = ((), (), s32[]{:S(2)}) async-start(), calls=%async_computation.16 | async-start | bytes 1310720 | tf_op jit(solution)/shard_map/reduce_scatter | solution.py:154
  273.6 26.3 %collective-permute-start.32 = (bf16[256,1024]{1,0:T(8,128)(2,1)S(1)}, bf16[256,1024]{1,0:T(8,128)(2,1)}, u32[]{:S(2)}, u32[]{:S(2)}) collective-permute-start(bf16[256,1024]{1,0:T(8,128)(2,1)S(1)} %add_convert_fusion.15), channel_id=1, source_target_pairs={{0,16},{4,20},{8,24},{12,28},{16,0},{20,4},{24,8},{28,12},{1,17},{... | collective-permute-start | bytes 1572872 | tf_op jit(solution)/shard_map/ppermute | solution.py:42
  275.8 27.4 %collective-permute-start.33 = (bf16[256,1024]{1,0:T(8,128)(2,1)S(1)}, bf16[256,1024]{1,0:T(8,128)(2,1)}, u32[]{:S(2)}, u32[]{:S(2)}) collective-permute-start(bf16[256,1024]{1,0:T(8,128)(2,1)S(1)} %add_convert_fusion.14), channel_id=1, source_target_pairs={{0,8},{4,12},{8,0},{12,4},{16,24},{20,28},{24,16},{28,20},{1,9},{5... | collective-permute-start | bytes 1572872 | tf_op jit(solution)/shard_map/ppermute | solution.py:42
  292.5 22.4 %collective-permute-start.43 = (bf16[256,1024]{1,0:T(8,128)(2,1)S(1)}, bf16[256,1024]{1,0:T(8,128)(2,1)S(1)}, u32[]{:S(2)}, u32[]{:S(2)}) collective-permute-start(bf16[256,1024]{1,0:T(8,128)(2,1)S(1)} %convolution_convert_fusion.11), channel_id=1, source_target_pairs={{0,16},{4,20},{8,24},{12,28},{16,0},{20,4},{24,8},{28,12},{1,17},{... | collective-permute-start | bytes 1572872 | tf_op jit(solution)/shard_map/ppermute | solution.py:42
  294.5 24.8 %collective-permute-start.42 = (bf16[256,1024]{1,0:T(8,128)(2,1)S(1)}, bf16[256,1024]{1,0:T(8,128)(2,1)S(1)}, u32[]{:S(2)}, u32[]{:S(2)}) collective-permute-start(bf16[256,1024]{1,0:T(8,128)(2,1)S(1)} %convolution_convert_fusion.9), channel_id=1, source_target_pairs={{0,8},{4,12},{8,0},{12,4},{16,24},{20,28},{24,16},{28,20},{1,9},{5... | collective-permute-start | bytes 1572872 | tf_op jit(solution)/shard_map/ppermute | solution.py:42
  299.9 34.2 %collective-permute-start.41 = (bf16[64,2048]{1,0:T(8,128)(2,1)S(1)}, bf16[64,2048]{1,0:T(8,128)(2,1)}, u32[]{:S(2)}, u32[]{:S(2)}) collective-permute-start(bf16[64,2048]{1,0:T(8,128)(2,1)S(1)} %fusion.24), channel_id=1, source_target_pairs={{0,3},{1,0},{2,1},{3,2},{4,7},{5,4},{6,5},{7,6},{8,11},{9,8},{10,9... | collective-permute-start | bytes 786440 | tf_op jit(solution)/shard_map/ppermute | solution.py:45
  304.5 39.7 %collective-permute-start.37 = (bf16[256,1024]{1,0:T(8,128)(2,1)S(1)}, bf16[256,1024]{1,0:T(8,128)(2,1)}, u32[]{:S(2)}, u32[]{:S(2)}) collective-permute-start(bf16[256,1024]{1,0:T(8,128)(2,1)S(1)} %add_convert_fusion.13), channel_id=1, source_target_pairs={{0,8},{4,12},{8,0},{12,4},{16,24},{20,28},{24,16},{28,20},{1,9},{5... | collective-permute-start | bytes 1572872 | tf_op jit(solution)/shard_map/ppermute | solution.py:42
  314.5 29.7 %collective-permute-start.38 = (bf16[256,1024]{1,0:T(8,128)(2,1)S(1)}, bf16[256,1024]{1,0:T(8,128)(2,1)}, u32[]{:S(2)}, u32[]{:S(2)}) collective-permute-start(bf16[256,1024]{1,0:T(8,128)(2,1)S(1)} %add_convert_fusion.12), channel_id=1, source_target_pairs={{0,16},{4,20},{8,24},{12,28},{16,0},{20,4},{24,8},{28,12},{1,17},{... | collective-permute-start | bytes 1572872 | tf_op jit(solution)/shard_map/ppermute | solution.py:42
  320.3 45.1 %collective-permute-start.45 = (bf16[256,1024]{1,0:T(8,128)(2,1)S(1)}, bf16[256,1024]{1,0:T(8,128)(2,1)}, u32[]{:S(2)}, u32[]{:S(2)}) collective-permute-start(bf16[256,1024]{1,0:T(8,128)(2,1)S(1)} %add_convert_fusion.11), channel_id=1, source_target_pairs={{0,8},{4,12},{8,0},{12,4},{16,24},{20,28},{24,16},{28,20},{1,9},{5... | collective-permute-start | bytes 1572872 | tf_op jit(solution)/shard_map/ppermute | solution.py:42
  340.7 27.5 %collective-permute-start.52 = (bf16[256,1024]{1,0:T(8,128)(2,1)}, bf16[256,1024]{1,0:T(8,128)(2,1)}, u32[]{:S(2)}, u32[]{:S(2)}) collective-permute-start(bf16[256,1024]{1,0:T(8,128)(2,1)} %convolution_convert_fusion.7), channel_id=1, source_target_pairs={{0,16},{4,20},{8,24},{12,28},{16,0},{20,4},{24,8},{28,12},{1,17},{... | collective-permute-start | bytes 1572872 | tf_op jit(solution)/shard_map/ppermute | solution.py:42
  360.6 114.5 %reduce-scatter.19.cloned.1.call-start = ((), (), s32[]{:S(2)}) async-start(), calls=%async_computation.17 | async-start | bytes 1310720 | tf_op jit(solution)/shard_map/reduce_scatter | solution.py:154
  366.8 45.8 %collective-permute-start.47 = (bf16[256,1024]{1,0:T(8,128)(2,1)S(1)}, bf16[256,1024]{1,0:T(8,128)(2,1)S(1)}, u32[]{:S(2)}, u32[]{:S(2)}) collective-permute-start(bf16[256,1024]{1,0:T(8,128)(2,1)S(1)} %add_convert_fusion.8), channel_id=1, source_target_pairs={{0,16},{4,20},{8,24},{12,28},{16,0},{20,4},{24,8},{28,12},{1,17},{... | collective-permute-start | bytes 1572872 | tf_op jit(solution)/shard_map/ppermute | solution.py:42
  369.6 51.5 %collective-permute-start.54 = (bf16[256,1024]{1,0:T(8,128)(2,1)S(1)}, bf16[256,1024]{1,0:T(8,128)(2,1)}, u32[]{:S(2)}, u32[]{:S(2)}) collective-permute-start(bf16[256,1024]{1,0:T(8,128)(2,1)S(1)} %add_convert_fusion.7), channel_id=1, source_target_pairs={{0,8},{4,12},{8,0},{12,4},{16,24},{20,28},{24,16},{28,20},{1,9},{5... | collective-permute-start | bytes 1572872 | tf_op jit(solution)/shard_map/ppermute | solution.py:42
  390.6 35.0 %collective-permute-start.58 = (bf16[256,1024]{1,0:T(8,128)(2,1)}, bf16[256,1024]{1,0:T(8,128)(2,1)}, u32[]{:S(2)}, u32[]{:S(2)}) collective-permute-start(bf16[256,1024]{1,0:T(8,128)(2,1)} %convolution_convert_fusion.3), channel_id=1, source_target_pairs={{0,16},{4,20},{8,24},{12,28},{16,0},{20,4},{24,8},{28,12},{1,17},{... | collective-permute-start | bytes 1572872 | tf_op jit(solution)/shard_map/ppermute | solution.py:42
  390.6 35.0 %collective-permute-start.57 = (bf16[256,1024]{1,0:T(8,128)(2,1)}, bf16[256,1024]{1,0:T(8,128)(2,1)}, u32[]{:S(2)}, u32[]{:S(2)}) collective-permute-start(bf16[256,1024]{1,0:T(8,128)(2,1)} %convolution_convert_fusion.1), channel_id=1, source_target_pairs={{0,8},{4,12},{8,0},{12,4},{16,24},{20,28},{24,16},{28,20},{1,9},{5... | collective-permute-start | bytes 1572872 | tf_op jit(solution)/shard_map/ppermute | solution.py:42
  390.8 20.7 %collective-permute-start.46 = (bf16[256,1024]{1,0:T(8,128)(2,1)S(1)}, bf16[256,1024]{1,0:T(8,128)(2,1)S(1)}, u32[]{:S(2)}, u32[]{:S(2)}) collective-permute-start(bf16[256,1024]{1,0:T(8,128)(2,1)S(1)} %add_convert_fusion.9), channel_id=1, source_target_pairs={{0,8},{4,12},{8,0},{12,4},{16,24},{20,28},{24,16},{28,20},{1,9},{5... | collective-permute-start | bytes 1572872 | tf_op jit(solution)/shard_map/ppermute | solution.py:42
  427.0 24.9 %collective-permute-start.60 = (bf16[256,1024]{1,0:T(8,128)(2,1)S(1)}, bf16[256,1024]{1,0:T(8,128)(2,1)}, u32[]{:S(2)}, u32[]{:S(2)}) collective-permute-start(bf16[256,1024]{1,0:T(8,128)(2,1)S(1)} %add_convert_fusion.3), channel_id=1, source_target_pairs={{0,8},{4,12},{8,0},{12,4},{16,24},{20,28},{24,16},{28,20},{1,9},{5... | collective-permute-start | bytes 1572872 | tf_op jit(solution)/shard_map/ppermute | solution.py:42
  428.5 23.4 %collective-permute-start.59 = (bf16[256,1024]{1,0:T(8,128)(2,1)S(1)}, bf16[256,1024]{1,0:T(8,128)(2,1)}, u32[]{:S(2)}, u32[]{:S(2)}) collective-permute-start(bf16[256,1024]{1,0:T(8,128)(2,1)S(1)} %add_convert_fusion.2), channel_id=1, source_target_pairs={{0,16},{4,20},{8,24},{12,28},{16,0},{20,4},{24,8},{28,12},{1,17},{... | collective-permute-start | bytes 1572872 | tf_op jit(solution)/shard_map/ppermute | solution.py:42
  430.3 61.5 %reduce-scatter.21.cloned.1.call-start = ((), (), s32[]{:S(2)}) async-start(), calls=%async_computation.18 | async-start | bytes 1310720 | tf_op jit(solution)/shard_map/reduce_scatter | solution.py:154
  455.2 65.2 %reduce-scatter.23.cloned.1.call-start = ((), (), s32[]{:S(2)}) async-start(), calls=%async_computation.19 | async-start | bytes 1310720 | tf_op jit(solution)/shard_map/reduce_scatter | solution.py:154
  (108 other events, 989.1 us)
Sparse Core Ops, SparseCore 0:
  16.2 30.5 all-gather.4
  48.4 27.3 all-gather.6
  77.3 27.3 all-gather.8
  106.2 27.3 all-gather.10
  172.0 26.4 reduce-scatter.8
  207.9 33.4 reduce-scatter.10
  250.6 35.6 reduce-scatter.12
  289.2 43.6 reduce-scatter.14
  360.7 32.2 reduce-scatter.16
  430.4 33.2 reduce-scatter.18
  466.0 25.7 reduce-scatter.20
  494.6 25.7 reduce-scatter.22

commit v2 on v1

--- a/solution.py
+++ b/solution.py
@@ -8,10 +8,10 @@
 SHARES = (4, 4, 4, 4)
 GATHERED = (0, 1, 2, 3)
 PLAN = (
-    "B0", "C0", "B1", "E0", "C1", "B2", "F0", "E1", "B3", "C2", "F1", "C3",
-    "G0", "E2", "E3", "A4", "F2", "G1", "B4", "F3", "A5", "C4", "G2", "B5",
-    "E4", "A6", "C5", "G3", "B6", "F4", "A7", "E5", "C6", "B7", "F5", "E6",
-    "C7", "F6", "E7", "F7",
+    "B0", "C0", "B1", "E0", "C1", "B2", "F0", "E1", "B3", "H0", "C2", "F1",
+    "C3", "G0", "E2", "H1", "E3", "A4", "F2", "G1", "B4", "H2", "F3", "A5",
+    "C4", "G2", "B5", "H3", "E4", "A6", "C5", "G3", "B6", "F4", "A7", "E5",
+    "C6", "B7", "F5", "E6", "C7", "F6", "E7", "F7",
 )
 
 
@@ -41,8 +41,10 @@
     def swap(v, mask):
         return lax.ppermute(v, "row", [(i, i ^ mask) for i in range(rows)])
 
-    def turn(v, step):
-        return lax.ppermute(v, "col", [(i, (i + step) % cols) for i in range(cols)])
+    def swap_col(v, mask):
+        return lax.ppermute(v, "col", [(i, i ^ mask) for i in range(cols)])
+
+    masks = [1 << b for b in range(cols.bit_length() - 1)][::-1]
 
     def on_device(rotation, gradient):
         me_row, me_col = lax.axis_index("row"), lax.axis_index("col")
@@ -85,19 +87,15 @@
             return tie(arrays, token[0])
 
         def start_panel(k, own):
-            state[k]["ups"], state[k]["downs"] = [own], [own]
-            state[k]["ups"].append(turn(own, 1))
-            if cols > 2:
-                state[k]["downs"].append(turn(own, -1))
+            state[k]["own"] = own
+            state[k]["pieces"] = {m: swap_col(own, m) for m in masks}
 
         def forward_panel(k):
-            s = state[k]
-            ups, downs = s["ups"], s["downs"]
-            while len(ups) + len(downs) < cols + 1:
-                if len(ups) <= len(downs):
-                    ups.append(turn(ups[-1], 1))
-                else:
-                    downs.append(turn(downs[-1], -1))
+            pieces = state[k]["pieces"]
+            for m in masks:
+                for low in [d for d in pieces if d & -d > m]:
+                    if low | m not in pieces:
+                        pieces[low | m] = swap_col(pieces[low], m)
 
         def multiply(k):
             s = state[k]
@@ -105,17 +103,11 @@
                 panel = lax.all_gather(bases[k], "col", axis=0, tiled=True)
                 (panel,) = step([panel])
             else:
-                ups, downs = s["ups"], s["downs"]
-                near = step(ups + downs[1:])
-                ups, downs = near[: len(ups)], [None] + near[len(ups) :]
-
-                def pick_piece(z, j):
-                    d = (z - j) % cols
-                    return ups[d] if d < len(ups) else downs[cols - d]
-
+                offsets = sorted(s["pieces"])
+                near = step([s["own"]] + [s["pieces"][d] for d in offsets])
                 panel = jnp.concatenate(
                     [
-                        lax.select_n(me_col, *[pick_piece(z, j) for z in range(cols)])
+                        lax.select_n(me_col, *[near[z ^ j] for z in range(cols)])
                         for j in range(cols)
                     ],
                     axis=0,
@@ -151,12 +143,43 @@
             full = lax.optimization_barrier(tuple(full))
             term = (mm(full[0], turned[1]) - mm(full[1], turned[0])).astype(bf16)
             token[0] = term
-            s["term"] = lax.psum_scatter(term, "col", scatter_dimension=0, tiled=True)
+            if k >= n:
+                s["term"] = lax.psum_scatter(term, "col", scatter_dimension=0, tiled=True)
+                return
+            wide = term.shape[0] // cols
+            s["rest"] = {
+                d: [lax.dynamic_slice_in_dim(term, (me_col ^ d) * wide, wide, axis=0)]
+                for d in range(cols)
+            }
+            hand_over(k, masks[-1])
+
+        def total(parts):
+            return sum(p.astype(f32) for p in parts)
+
+        def hand_over(k, m):
+            rest = state[k]["rest"]
+            gone = [d for d in sorted(rest) if d & m]
+            sent = jnp.concatenate([total(rest.pop(d)).astype(bf16) for d in gone], axis=0)
+            state[k]["came"] = (gone, m, swap_col(sent, m))
+            token[0] = sent
+
+        def take(k):
+            s = state[k]
+            gone, m, got = s["came"]
+            (got,) = step([got])
+            wide = got.shape[0] // len(gone)
+            for i, d in enumerate(gone):
+                s["rest"][d ^ m].append(got[i * wide : (i + 1) * wide])
+
+        def halve(k):
+            for m in masks[-2::-1]:
+                take(k)
+                hand_over(k, m)
 
         def middle(k):
-            (term,) = step([state[k]["term"]])
+            take(k)
             wide = bases[k].astype(f32)
-            mid = (wide + (wide + 0.25 * term.astype(f32))).astype(bf16)
+            mid = (wide + (wide + 0.25 * total(state[k]["rest"][0]))).astype(bf16)
             token[0] = mid
             start_panel(k + n, mid)
 
@@ -176,6 +199,7 @@
             "E": lambda k: exchange(k, 0),
             "F": finish,
             "G": middle,
+            "H": halve,
         }
         for k in range(n):
             if k not in GATHERED:

time: 551 us -> 535 us (0.971)
  matrix products: 136 us -> 129 us
    reduce_scatter x8 -> x4, waiting for transfers between devices: 61.4 us -> 38.2 us  [finish(): s['term'] = lax.psum_scatter(term, 'col', scatter_dimension=0, tiled=True)]
    ppermute x12 -> x20, waiting for transfers between devices: 18.8 us -> 39.9 us  [swap_col(): return lax.ppermute(v, 'col', [(i, i ^ mask) for i in range(cols)])]
    ppermute x56, starting transfers between devices: 65.7 us -> 55.7 us  [swap(): return lax.ppermute(v, 'row', [(i, i ^ mask) for i in range(rows)])]
    dot_general x48, matrix products: 131 us -> 124 us  [mm(): lax.dot_general(a, b, (((1,), (0,)), ((), ())), preferred_element_type=f32)]
    ppermute x12 -> x20, starting transfers between devices: 21.3 us -> 26.5 us  [swap_col(): return lax.ppermute(v, 'col', [(i, i ^ mask) for i in range(cols)])]
  transfers between devices with their start and end apart: 80 -> 84, of which waited for: 31 -> 33; matrix products, arithmetic and copies ran while one was open for 41% -> 41% of each run, Pallas kernels for 0% -> 0%
where the time goes in v2:
time: 535 us; the launch traced here: 527 us
  waiting for transfers between devices  194 us (36%)
  matrix products  129 us (24%)
  other arithmetic  87.8 us (16%)
  starting transfers between devices  83.1 us (16%)
  local copies, waits for them, and re-layouts  17.9 us (3%)
  between operations  16 us (3%)
    dot_general x48, matrix products, mm(): lax.dot_general(a, b, (((1,), (0,)), ((), ())), preferred_element_type=f32)  124 us
    ppermute x56, waiting for transfers between devices, swap(): return lax.ppermute(v, 'row', [(i, i ^ mask) for i in range(rows)])  113 us
    ppermute x56, starting transfers between devices, swap(): return lax.ppermute(v, 'row', [(i, i ^ mask) for i in range(rows)])  55.7 us
    ppermute x20, waiting for transfers between devices, swap_col(): return lax.ppermute(v, 'col', [(i, i ^ mask) for i in range(cols)])  39.9 us
    reduce_scatter x4, waiting for transfers between devices, finish(): s['term'] = lax.psum_scatter(term, 'col', scatter_dimension=0, tiled=True)  38.2 us
    ppermute x20, starting transfers between devices, swap_col(): return lax.ppermute(v, 'col', [(i, i ^ mask) for i in range(cols)])  26.5 us
    convert_element_type x32, other arithmetic, exchange(): (flat[i].astype(f32) + flat[2 + i].astype(f32)).astype(bf16)  24.6 us
    transpose x2, other arithmetic, on_device(): turned = list(lax.optimization_barrier(tuple((w.T for w in weights))))  17 us
  transfers between devices with their start and end apart: 84, of which 33 were waited for; matrix products, arithmetic and copies ran while one was open for 41% of the time, Pallas kernels for 0%

profile of v2, /device:TPU:0, one launch (start us, length us, event | category | flops | bytes accessed | tf_op | source)
XLA Modules:
  0.0 527.1 jit_solution(2554084281023475971)
XLA Ops:
  7.3 4.6 fusion.19
  16.1 2.7 constant_dynamic-slice_fusion.9
  18.8 2.4 pad_maximum_fusion.3
  21.6 2.7 constant_dynamic-slice_fusion.11
  24.3 2.5 pad_maximum_fusion.2
  28.7 8.5 %fusion = bf16[2048,2048]{0,1:T(8,128)(2,1)} fusion(bf16[1024,2048]{1,0:T(8,128)(2,1)} %collective-permute-done.2, bf16[1024,2048]{1,0:T(8,128)(2,1)} %pad_maximum_fusion.3), kind=kLoop, calls=%fused_computation.10 | loop fusion | flops 16777216 | bytes 16777216 | tf_op jit(solution)/shard_map/transpose | solution.py:80
  37.3 8.5 %fusion.1 = bf16[2048,2048]{0,1:T(8,128)(2,1)} fusion(bf16[1024,2048]{1,0:T(8,128)(2,1)} %collective-permute-done.1, bf16[1024,2048]{1,0:T(8,128)(2,1)} %pad_maximum_fusion.2), kind=kLoop, calls=%fused_computation.11 | loop fusion | flops 16777216 | bytes 16777216 | tf_op jit(solution)/shard_map/transpose | solution.py:80
  46.8 4.2 fusion.3
  54.9 4.4 fusion.5
  67.1 7.3 %collective-permute-done.3 = bf16[256,1024]{1,0:T(8,128)(2,1)S(1)} collective-permute-done((bf16[256,1024]{1,0:T(8,128)(2,1)S(1)}, bf16[256,1024]{1,0:T(8,128)(2,1)S(1)}, u32[]{:S(2)}, u32[]{:S(2)}) %collective-permute-start.3) | collective-permute-done | bytes 524320 | tf_op jit(solution)/shard_map/ppermute | solution.py:42
  76.2 3.9 convolution_convert_fusion.27
  87.6 18.0 %collective-permute-done.5 = bf16[256,1024]{1,0:T(8,128)(2,1)S(1)} collective-permute-done((bf16[256,1024]{1,0:T(8,128)(2,1)S(1)}, bf16[256,1024]{1,0:T(8,128)(2,1)S(1)}, u32[]{:S(2)}, u32[]{:S(2)}) %collective-permute-start.5) | collective-permute-done | bytes 524320 | tf_op jit(solution)/shard_map/ppermute | solution.py:42
  109.9 4.8 convolution_convert_fusion.23
  124.2 18.8 %collective-permute-done.7 = bf16[256,1024]{1,0:T(8,128)(2,1)S(1)} collective-permute-done((bf16[256,1024]{1,0:T(8,128)(2,1)S(1)}, bf16[256,1024]{1,0:T(8,128)(2,1)S(1)}, u32[]{:S(2)}, u32[]{:S(2)}) %collective-permute-start.7) | collective-permute-done | bytes 524320 | tf_op jit(solution)/shard_map/ppermute | solution.py:42
  143.8 2.4 fusion.33
  151.6 2.8 collective-permute-done.12
  156.1 4.7 convolution_convert_fusion.21
  175.6 8.3 %collective-permute-done.17 = bf16[256,1024]{1,0:T(8,128)(2,1)S(1)} collective-permute-done((bf16[256,1024]{1,0:T(8,128)(2,1)S(1)}, bf16[256,1024]{1,0:T(8,128)(2,1)S(1)}, u32[]{:S(2)}, u32[]{:S(2)}) %collective-permute-start.17) | collective-permute-done | bytes 524320 | tf_op jit(solution)/shard_map/ppermute | solution.py:42
  186.8 4.1 fusion.34
  190.9 4.0 fusion.8
  204.0 6.8 %collective-permute-done.25 = bf16[256,1024]{1,0:T(8,128)(2,1)S(1)} collective-permute-done((bf16[256,1024]{1,0:T(8,128)(2,1)S(1)}, bf16[256,1024]{1,0:T(8,128)(2,1)S(1)}, u32[]{:S(2)}, u32[]{:S(2)}) %collective-permute-start.25) | collective-permute-done | bytes 524320 | tf_op jit(solution)/shard_map/ppermute | solution.py:42
  217.8 3.9 collective-permute-done.30
  224.6 7.7 %collective-permute-done.28 = bf16[256,1024]{1,0:T(8,128)(2,1)S(1)} collective-permute-done((bf16[256,1024]{1,0:T(8,128)(2,1)S(1)}, bf16[256,1024]{1,0:T(8,128)(2,1)S(1)}, u32[]{:S(2)}, u32[]{:S(2)}) %collective-permute-start.28) | collective-permute-done | bytes 524320 | tf_op jit(solution)/shard_map/ppermute | solution.py:42
  235.0 3.7 fusion.35
  238.7 4.3 fusion.9
  257.6 8.2 %collective-permute-done.36 = bf16[128,2048]{1,0:T(8,128)(2,1)S(1)} collective-permute-done((bf16[128,2048]{1,0:T(8,128)(2,1)S(1)}, bf16[128,2048]{1,0:T(8,128)(2,1)S(1)}, u32[]{:S(2)}, u32[]{:S(2)}) %collective-permute-start.36) | collective-permute-done | bytes 524320 | tf_op jit(solution)/shard_map/ppermute | solution.py:45
  266.8 2.5 collective-permute-start.40
  269.3 5.2 collective-permute-done.41
  274.6 3.3 collective-permute-start.42
  281.3 3.7 fusion.36
  285.0 4.0 fusion.10
  305.5 3.0 collective-permute-start.47
  311.0 4.8 collective-permute-done.47
  321.4 4.4 collective-permute-done.49
  345.8 3.3 fusion.11
  352.2 2.9 collective-permute-done.52
  360.8 14.1 %collective-permute-done.58 = bf16[64,2048]{1,0:T(8,128)(2,1)S(1)} collective-permute-done((bf16[64,2048]{1,0:T(8,128)(2,1)S(1)}, bf16[64,2048]{1,0:T(8,128)(2,1)S(1)}, u32[]{:S(2)}, u32[]{:S(2)}) %collective-permute-start.58) | collective-permute-done | bytes 262176 | tf_op jit(solution)/shard_map/ppermute | solution.py:45
  387.1 10.6 %collective-permute-done.54 = bf16[256,1024]{1,0:T(8,128)(2,1)S(1)} collective-permute-done((bf16[256,1024]{1,0:T(8,128)(2,1)S(1)}, bf16[256,1024]{1,0:T(8,128)(2,1)S(1)}, u32[]{:S(2)}, u32[]{:S(2)}) %collective-permute-start.54) | collective-permute-done | bytes 524320 | tf_op jit(solution)/shard_map/ppermute | solution.py:42
  402.2 3.3 fusion.12
  405.5 4.4 collective-permute-done.61
  419.6 3.3 collective-permute-done.64
  425.5 5.9 %fusion.39 = f32[256,2048]{1,0:T(8,128)S(1)} fusion(bf16[256,2048]{1,0:T(8,128)(2,1)S(1)} %pad_maximum_fusion.21, bf16[2048,2048]{0,1:T(8,128)(2,1)} %fusion.1), kind=kOutput, calls=%fused_computation.242 | convolution fusion | flops 2147483648 | bytes 11534336 | tf_op jit(solution)/shard_map/dot_general | solution.py:22
  431.4 3.3 fusion.13
  439.4 5.9 %collective-permute-done.70 = bf16[256,1024]{1,0:T(8,128)(2,1)S(1)} collective-permute-done((bf16[256,1024]{1,0:T(8,128)(2,1)S(1)}, bf16[256,1024]{1,0:T(8,128)(2,1)S(1)}, u32[]{:S(2)}, u32[]{:S(2)}) %collective-permute-start.70) | collective-permute-done | bytes 524320 | tf_op jit(solution)/shard_map/ppermute | solution.py:42
  450.6 6.0 %fusion.40 = f32[256,2048]{1,0:T(8,128)S(1)} fusion(bf16[256,2048]{1,0:T(8,128)(2,1)S(1)} %pad_maximum_fusion.23, bf16[2048,2048]{0,1:T(8,128)(2,1)} %fusion.1), kind=kOutput, calls=%fused_computation.243 | convolution fusion | flops 2147483648 | bytes 11534336 | tf_op jit(solution)/shard_map/dot_general | solution.py:22
  456.7 3.3 fusion.14
  463.4 11.6 %reduce-scatter.9.cloned.1.call-done = bf16[64,2048]{1,0:T(8,128)(2,1)} async-done(((bf16[256,2048]{1,0:T(8,128)(2,1)}), bf16[64,2048]{1,0:T(8,128)(2,1)}) %reduce-scatter.9.cloned.1.call-update) | async-done | bytes 262160 | tf_op jit(solution)/shard_map/reduce_scatter | solution.py:147
  477.1 26.6 %reduce-scatter.11.cloned.1.call-done = bf16[64,2048]{1,0:T(8,128)(2,1)} async-done(((bf16[256,2048]{1,0:T(8,128)(2,1)}), bf16[64,2048]{1,0:T(8,128)(2,1)}) %reduce-scatter.11.cloned.1.call-update) | async-done | bytes 262160 | tf_op jit(solution)/shard_map/reduce_scatter | solution.py:147
  (433 shorter events, 221.3 us)
Async XLA Ops:
  7.2 39.7 %all-gather.5.cloned.1.call-start = ((), (), s32[]{:S(2)}) async-start(), calls=%async_computation.4 | async-start | bytes 1310720 | tf_op jit(solution)/shard_map/all_gather | solution.py:103
  16.1 60.1 %all-gather.7.cloned.1.call-start = ((), (), s32[]{:S(2)}) async-start(), calls=%async_computation.5 | async-start | bytes 1310720 | tf_op jit(solution)/shard_map/all_gather | solution.py:103
  27.0 82.9 %all-gather.9.cloned.1.call-start = ((), (), s32[]{:S(2)}) async-start(), calls=%async_computation.6 | async-start | bytes 1310720 | tf_op jit(solution)/shard_map/all_gather | solution.py:103
  27.7 128.4 %all-gather.11.cloned.1.call-start = ((), (), s32[]{:S(2)}) async-start(), calls=%async_computation.7 | async-start | bytes 1310720 | tf_op jit(solution)/shard_map/all_gather | solution.py:103
  28.3 431.8 %reduce-scatter.5.cloned.1.call-start = ((), (), s32[]{:S(2)}) async-start(), calls=%async_computation.8 | async-start | bytes 1310720 | tf_op jit(solution)/shard_map/reduce_scatter | solution.py:147
  74.6 31.8 %collective-permute-start.6 = (bf16[256,1024]{1,0:T(8,128)(2,1)S(1)}, bf16[256,1024]{1,0:T(8,128)(2,1)S(1)}, u32[]{:S(2)}, u32[]{:S(2)}) collective-permute-start(bf16[256,1024]{1,0:T(8,128)(2,1)S(1)} %add_convert_fusion.30), channel_id=1, source_target_pairs={{0,8},{4,12},{8,0},{12,4},{16,24},{20,28},{24,16},{28,20},{1,9},{5... | collective-permute-start | bytes 1572872 | tf_op jit(solution)/shard_map/ppermute | solution.py:42
  81.5 26.6 %collective-permute-start.10 = (bf16[256,1024]{1,0:T(8,128)(2,1)S(1)}, bf16[256,1024]{1,0:T(8,128)(2,1)S(1)}, u32[]{:S(2)}, u32[]{:S(2)}) collective-permute-start(bf16[256,1024]{1,0:T(8,128)(2,1)S(1)} %convolution_convert_fusion.27), channel_id=1, source_target_pairs={{0,16},{4,20},{8,24},{12,28},{16,0},{20,4},{24,8},{28,12},{1,17},{... | collective-permute-start | bytes 1572872 | tf_op jit(solution)/shard_map/ppermute | solution.py:42
  82.9 22.7 %collective-permute-start.5 = (bf16[256,1024]{1,0:T(8,128)(2,1)S(1)}, bf16[256,1024]{1,0:T(8,128)(2,1)S(1)}, u32[]{:S(2)}, u32[]{:S(2)}) collective-permute-start(bf16[256,1024]{1,0:T(8,128)(2,1)S(1)} %add_convert_fusion.31), channel_id=1, source_target_pairs={{0,16},{4,20},{8,24},{12,28},{16,0},{20,4},{24,8},{28,12},{1,17},{... | collective-permute-start | bytes 1572872 | tf_op jit(solution)/shard_map/ppermute | solution.py:42
  85.2 23.0 %collective-permute-start.9 = (bf16[256,1024]{1,0:T(8,128)(2,1)S(1)}, bf16[256,1024]{1,0:T(8,128)(2,1)S(1)}, u32[]{:S(2)}, u32[]{:S(2)}) collective-permute-start(bf16[256,1024]{1,0:T(8,128)(2,1)S(1)} %convolution_convert_fusion.25), channel_id=1, source_target_pairs={{0,8},{4,12},{8,0},{12,4},{16,24},{20,28},{24,16},{28,20},{1,9},{5... | collective-permute-start | bytes 1572872 | tf_op jit(solution)/shard_map/ppermute | solution.py:42
  106.6 36.7 %collective-permute-start.8 = (bf16[256,1024]{1,0:T(8,128)(2,1)S(1)}, bf16[256,1024]{1,0:T(8,128)(2,1)S(1)}, u32[]{:S(2)}, u32[]{:S(2)}) collective-permute-start(bf16[256,1024]{1,0:T(8,128)(2,1)S(1)} %add_convert_fusion.28), channel_id=1, source_target_pairs={{0,16},{4,20},{8,24},{12,28},{16,0},{20,4},{24,8},{28,12},{1,17},{... | collective-permute-start | bytes 1572872 | tf_op jit(solution)/shard_map/ppermute | solution.py:42
  108.4 43.2 %collective-permute-start.13 = (bf16[256,1024]{1,0:T(8,128)(2,1)S(1)}, bf16[256,1024]{1,0:T(8,128)(2,1)}, u32[]{:S(2)}, u32[]{:S(2)}) collective-permute-start(bf16[256,1024]{1,0:T(8,128)(2,1)S(1)} %add_convert_fusion.27), channel_id=1, source_target_pairs={{0,8},{4,12},{8,0},{12,4},{16,24},{20,28},{24,16},{28,20},{1,9},{5... | collective-permute-start | bytes 1572872 | tf_op jit(solution)/shard_map/ppermute | solution.py:42
  116.8 55.5 %collective-permute-start.19 = (bf16[256,1024]{1,0:T(8,128)(2,1)}, bf16[256,1024]{1,0:T(8,128)(2,1)}, u32[]{:S(2)}, u32[]{:S(2)}) collective-permute-start(bf16[256,1024]{1,0:T(8,128)(2,1)} %convolution_convert_fusion.17), channel_id=1, source_target_pairs={{0,8},{4,12},{8,0},{12,4},{16,24},{20,28},{24,16},{28,20},{1,9},{5... | collective-permute-start | bytes 1572872 | tf_op jit(solution)/shard_map/ppermute | solution.py:42
  117.3 55.6 %collective-permute-start.20 = (bf16[256,1024]{1,0:T(8,128)(2,1)}, bf16[256,1024]{1,0:T(8,128)(2,1)}, u32[]{:S(2)}, u32[]{:S(2)}) collective-permute-start(bf16[256,1024]{1,0:T(8,128)(2,1)} %convolution_convert_fusion.23), channel_id=1, source_target_pairs={{0,16},{4,20},{8,24},{12,28},{16,0},{20,4},{24,8},{28,12},{1,17},{... | collective-permute-start | bytes 1572872 | tf_op jit(solution)/shard_map/ppermute | solution.py:42
  120.1 22.9 %collective-permute-start.7 = (bf16[256,1024]{1,0:T(8,128)(2,1)S(1)}, bf16[256,1024]{1,0:T(8,128)(2,1)S(1)}, u32[]{:S(2)}, u32[]{:S(2)}) collective-permute-start(bf16[256,1024]{1,0:T(8,128)(2,1)S(1)} %add_convert_fusion.29), channel_id=1, source_target_pairs={{0,8},{4,12},{8,0},{12,4},{16,24},{20,28},{24,16},{28,20},{1,9},{5... | collective-permute-start | bytes 1572872 | tf_op jit(solution)/shard_map/ppermute | solution.py:42
  150.4 18.7 %collective-permute-start.11 = (bf16[128,2048]{1,0:T(8,128)(2,1)}, bf16[128,2048]{1,0:T(8,128)(2,1)}, u32[]{:S(2)}, u32[]{:S(2)}) collective-permute-start(bf16[128,2048]{1,0:T(8,128)(2,1)} %pad_maximum_fusion.25), channel_id=1, source_target_pairs={{0,1},{1,0},{2,3},{3,2},{4,5},{5,4},{6,7},{7,6},{8,9},{9,8},{10,11... | collective-permute-start | bytes 1572872 | tf_op jit(solution)/shard_map/ppermute | solution.py:45
  155.8 29.6 %collective-permute-start.18 = (bf16[256,1024]{1,0:T(8,128)(2,1)S(1)}, bf16[256,1024]{1,0:T(8,128)(2,1)}, u32[]{:S(2)}, u32[]{:S(2)}) collective-permute-start(bf16[256,1024]{1,0:T(8,128)(2,1)S(1)} %add_convert_fusion.25), channel_id=1, source_target_pairs={{0,16},{4,20},{8,24},{12,28},{16,0},{20,4},{24,8},{28,12},{1,17},{... | collective-permute-start | bytes 1572872 | tf_op jit(solution)/shard_map/ppermute | solution.py:42
  162.9 32.5 %collective-permute-start.16 = (bf16[256,1024]{1,0:T(8,128)(2,1)}, bf16[256,1024]{1,0:T(8,128)(2,1)}, u32[]{:S(2)}, u32[]{:S(2)}) collective-permute-start(bf16[256,1024]{1,0:T(8,128)(2,1)} %convolution_convert_fusion.21), channel_id=1, source_target_pairs={{0,16},{4,20},{8,24},{12,28},{16,0},{20,4},{24,8},{28,12},{1,17},{... | collective-permute-start | bytes 1572872 | tf_op jit(solution)/shard_map/ppermute | solution.py:42
  172.3 23.1 %collective-permute-start.15 = (bf16[256,1024]{1,0:T(8,128)(2,1)}, bf16[256,1024]{1,0:T(8,128)(2,1)}, u32[]{:S(2)}, u32[]{:S(2)}) collective-permute-start(bf16[256,1024]{1,0:T(8,128)(2,1)} %convolution_convert_fusion.19), channel_id=1, source_target_pairs={{0,8},{4,12},{8,0},{12,4},{16,24},{20,28},{24,16},{28,20},{1,9},{5... | collective-permute-start | bytes 1572872 | tf_op jit(solution)/shard_map/ppermute | solution.py:42
  172.9 28.4 %collective-permute-start.14 = (bf16[64,2048]{1,0:T(8,128)(2,1)}, bf16[64,2048]{1,0:T(8,128)(2,1)S(1)}, u32[]{:S(2)}, u32[]{:S(2)}) collective-permute-start(bf16[64,2048]{1,0:T(8,128)(2,1)} %add_convert_fusion.35), channel_id=1, source_target_pairs={{0,2},{1,3},{2,0},{3,1},{4,6},{5,7},{6,4},{7,5},{8,10},{9,11},{10,... | collective-permute-start | bytes 786440 | tf_op jit(solution)/shard_map/ppermute | solution.py:45
  183.9 29.1 %collective-permute-start.26 = (bf16[256,1024]{1,0:T(8,128)(2,1)S(1)}, bf16[256,1024]{1,0:T(8,128)(2,1)}, u32[]{:S(2)}, u32[]{:S(2)}) collective-permute-start(bf16[256,1024]{1,0:T(8,128)(2,1)S(1)} %add_convert_fusion.23), channel_id=1, source_target_pairs={{0,8},{4,12},{8,0},{12,4},{16,24},{20,28},{24,16},{28,20},{1,9},{5... | collective-permute-start | bytes 1572872 | tf_op jit(solution)/shard_map/ppermute | solution.py:42
  195.1 21.2 %collective-permute-start.24 = (bf16[128,2048]{1,0:T(8,128)(2,1)S(1)}, bf16[128,2048]{1,0:T(8,128)(2,1)S(1)}, u32[]{:S(2)}, u32[]{:S(2)}) collective-permute-start(bf16[128,2048]{1,0:T(8,128)(2,1)S(1)} %pad_maximum_fusion.26), channel_id=1, source_target_pairs={{0,1},{1,0},{2,3},{3,2},{4,5},{5,4},{6,7},{7,6},{8,9},{9,8},{10,11... | collective-permute-start | bytes 1572872 | tf_op jit(solution)/shard_map/ppermute | solution.py:45
  198.7 19.1 %collective-permute-start.31 = (bf16[256,1024]{1,0:T(8,128)(2,1)S(1)}, bf16[256,1024]{1,0:T(8,128)(2,1)S(1)}, u32[]{:S(2)}, u32[]{:S(2)}) collective-permute-start(bf16[256,1024]{1,0:T(8,128)(2,1)S(1)} %add_convert_fusion.22), channel_id=1, source_target_pairs={{0,8},{4,12},{8,0},{12,4},{16,24},{20,28},{24,16},{28,20},{1,9},{5... | collective-permute-start | bytes 1572872 | tf_op jit(solution)/shard_map/ppermute | solution.py:42
  201.3 20.4 %collective-permute-start.30 = (bf16[256,1024]{1,0:T(8,128)(2,1)S(1)}, bf16[256,1024]{1,0:T(8,128)(2,1)S(1)}, u32[]{:S(2)}, u32[]{:S(2)}) collective-permute-start(bf16[256,1024]{1,0:T(8,128)(2,1)S(1)} %add_convert_fusion.18), channel_id=1, source_target_pairs={{0,16},{4,20},{8,24},{12,28},{16,0},{20,4},{24,8},{28,12},{1,17},{... | collective-permute-start | bytes 1572872 | tf_op jit(solution)/shard_map/ppermute | solution.py:42
  213.1 31.4 %collective-permute-start.21 = (bf16[64,2048]{1,0:T(8,128)(2,1)S(1)}, bf16[64,2048]{1,0:T(8,128)(2,1)}, u32[]{:S(2)}, u32[]{:S(2)}) collective-permute-start(bf16[64,2048]{1,0:T(8,128)(2,1)S(1)} %fusion.22), channel_id=1, source_target_pairs={{0,1},{1,0},{2,3},{3,2},{4,5},{5,4},{6,7},{7,6},{8,9},{9,8},{10,11... | collective-permute-start | bytes 786440 | tf_op jit(solution)/shard_map/ppermute | solution.py:45
  221.7 21.4 %collective-permute-start.27 = (bf16[64,2048]{1,0:T(8,128)(2,1)}, bf16[64,2048]{1,0:T(8,128)(2,1)}, u32[]{:S(2)}, u32[]{:S(2)}) collective-permute-start(bf16[64,2048]{1,0:T(8,128)(2,1)} %add_convert_fusion.34), channel_id=1, source_target_pairs={{0,2},{1,3},{2,0},{3,1},{4,6},{5,7},{6,4},{7,5},{8,10},{9,11},{10,... | collective-permute-start | bytes 786440 | tf_op jit(solution)/shard_map/ppermute | solution.py:45
  224.4 42.5 %collective-permute-start.35 = (bf16[256,1024]{1,0:T(8,128)(2,1)S(1)}, bf16[256,1024]{1,0:T(8,128)(2,1)}, u32[]{:S(2)}, u32[]{:S(2)}) collective-permute-start(bf16[256,1024]{1,0:T(8,128)(2,1)S(1)} %add_convert_fusion.17), channel_id=1, source_target_pairs={{0,16},{4,20},{8,24},{12,28},{16,0},{20,4},{24,8},{28,12},{1,17},{... | collective-permute-start | bytes 1572872 | tf_op jit(solution)/shard_map/ppermute | solution.py:42
  232.4 45.5 %collective-permute-start.34 = (bf16[256,1024]{1,0:T(8,128)(2,1)S(1)}, bf16[256,1024]{1,0:T(8,128)(2,1)}, u32[]{:S(2)}, u32[]{:S(2)}) collective-permute-start(bf16[256,1024]{1,0:T(8,128)(2,1)S(1)} %add_convert_fusion.16), channel_id=1, source_target_pairs={{0,8},{4,12},{8,0},{12,4},{16,24},{20,28},{24,16},{28,20},{1,9},{5... | collective-permute-start | bytes 1572872 | tf_op jit(solution)/shard_map/ppermute | solution.py:42
  250.2 38.9 %collective-permute-start.32 = (bf16[256,1024]{1,0:T(8,128)(2,1)}, bf16[256,1024]{1,0:T(8,128)(2,1)}, u32[]{:S(2)}, u32[]{:S(2)}) collective-permute-start(bf16[256,1024]{1,0:T(8,128)(2,1)} %convolution_convert_fusion.15), channel_id=1, source_target_pairs={{0,8},{4,12},{8,0},{12,4},{16,24},{20,28},{24,16},{28,20},{1,9},{5... | collective-permute-start | bytes 1572872 | tf_op jit(solution)/shard_map/ppermute | solution.py:42
  255.1 34.0 %collective-permute-start.33 = (bf16[256,1024]{1,0:T(8,128)(2,1)}, bf16[256,1024]{1,0:T(8,128)(2,1)}, u32[]{:S(2)}, u32[]{:S(2)}) collective-permute-start(bf16[256,1024]{1,0:T(8,128)(2,1)} %convolution_convert_fusion.14), channel_id=1, source_target_pairs={{0,16},{4,20},{8,24},{12,28},{16,0},{20,4},{24,8},{28,12},{1,17},{... | collective-permute-start | bytes 1572872 | tf_op jit(solution)/shard_map/ppermute | solution.py:42
  266.8 29.8 %collective-permute-start.40 = (bf16[64,2048]{1,0:T(8,128)(2,1)S(1)}, bf16[64,2048]{1,0:T(8,128)(2,1)}, u32[]{:S(2)}, u32[]{:S(2)}) collective-permute-start(bf16[64,2048]{1,0:T(8,128)(2,1)S(1)} %fusion.23), channel_id=1, source_target_pairs={{0,1},{1,0},{2,3},{3,2},{4,5},{5,4},{6,7},{7,6},{8,9},{9,8},{10,11... | collective-permute-start | bytes 786440 | tf_op jit(solution)/shard_map/ppermute | solution.py:45
  274.6 22.1 %collective-permute-start.42 = (bf16[64,2048]{1,0:T(8,128)(2,1)S(1)}, bf16[64,2048]{1,0:T(8,128)(2,1)}, u32[]{:S(2)}, u32[]{:S(2)}) collective-permute-start(bf16[64,2048]{1,0:T(8,128)(2,1)S(1)} %collective-permute-done.41), channel_id=1, source_target_pairs={{0,1},{1,0},{2,3},{3,2},{4,5},{5,4},{6,7},{7,6},{8,9},{9,8},{10,11... | collective-permute-start | bytes 786440 | tf_op jit(solution)/shard_map/ppermute | solution.py:45
  291.1 17.5 %collective-permute-start.37 = (bf16[256,1024]{1,0:T(8,128)(2,1)S(1)}, bf16[256,1024]{1,0:T(8,128)(2,1)S(1)}, u32[]{:S(2)}, u32[]{:S(2)}) collective-permute-start(bf16[256,1024]{1,0:T(8,128)(2,1)S(1)} %add_convert_fusion.15), channel_id=1, source_target_pairs={{0,16},{4,20},{8,24},{12,28},{16,0},{20,4},{24,8},{28,12},{1,17},{... | collective-permute-start | bytes 1572872 | tf_op jit(solution)/shard_map/ppermute | solution.py:42
  301.4 19.3 %collective-permute-start.51 = (bf16[256,1024]{1,0:T(8,128)(2,1)S(1)}, bf16[256,1024]{1,0:T(8,128)(2,1)S(1)}, u32[]{:S(2)}, u32[]{:S(2)}) collective-permute-start(bf16[256,1024]{1,0:T(8,128)(2,1)S(1)} %convolution_convert_fusion.11), channel_id=1, source_target_pairs={{0,16},{4,20},{8,24},{12,28},{16,0},{20,4},{24,8},{28,12},{1,17},{... | collective-permute-start | bytes 1572872 | tf_op jit(solution)/shard_map/ppermute | solution.py:42
  308.6 19.7 %collective-permute-start.46 = (bf16[64,2048]{1,0:T(8,128)(2,1)S(1)}, bf16[64,2048]{1,0:T(8,128)(2,1)S(1)}, u32[]{:S(2)}, u32[]{:S(2)}) collective-permute-start(bf16[64,2048]{1,0:T(8,128)(2,1)S(1)} %fusion.24), channel_id=1, source_target_pairs={{0,1},{1,0},{2,3},{3,2},{4,5},{5,4},{6,7},{7,6},{8,9},{9,8},{10,11... | collective-permute-start | bytes 786440 | tf_op jit(solution)/shard_map/ppermute | solution.py:45
  315.7 25.9 %collective-permute-start.44 = (bf16[256,1024]{1,0:T(8,128)(2,1)S(1)}, bf16[256,1024]{1,0:T(8,128)(2,1)S(1)}, u32[]{:S(2)}, u32[]{:S(2)}) collective-permute-start(bf16[256,1024]{1,0:T(8,128)(2,1)S(1)} %add_convert_fusion.13), channel_id=1, source_target_pairs={{0,8},{4,12},{8,0},{12,4},{16,24},{20,28},{24,16},{28,20},{1,9},{5... | collective-permute-start | bytes 1572872 | tf_op jit(solution)/shard_map/ppermute | solution.py:42
  319.1 23.0 %collective-permute-start.45 = (bf16[256,1024]{1,0:T(8,128)(2,1)S(1)}, bf16[256,1024]{1,0:T(8,128)(2,1)S(1)}, u32[]{:S(2)}, u32[]{:S(2)}) collective-permute-start(bf16[256,1024]{1,0:T(8,128)(2,1)S(1)} %add_convert_fusion.12), channel_id=1, source_target_pairs={{0,16},{4,20},{8,24},{12,28},{16,0},{20,4},{24,8},{28,12},{1,17},{... | collective-permute-start | bytes 1572872 | tf_op jit(solution)/shard_map/ppermute | solution.py:42
  325.8 30.2 %collective-permute-start.53 = (bf16[256,1024]{1,0:T(8,128)(2,1)S(1)}, bf16[256,1024]{1,0:T(8,128)(2,1)}, u32[]{:S(2)}, u32[]{:S(2)}) collective-permute-start(bf16[256,1024]{1,0:T(8,128)(2,1)S(1)} %add_convert_fusion.11), channel_id=1, source_target_pairs={{0,8},{4,12},{8,0},{12,4},{16,24},{20,28},{24,16},{28,20},{1,9},{5... | collective-permute-start | bytes 1572872 | tf_op jit(solution)/shard_map/ppermute | solution.py:42
  334.4 23.7 %collective-permute-start.60 = (bf16[256,1024]{1,0:T(8,128)(2,1)}, bf16[256,1024]{1,0:T(8,128)(2,1)}, u32[]{:S(2)}, u32[]{:S(2)}) collective-permute-start(bf16[256,1024]{1,0:T(8,128)(2,1)} %convolution_convert_fusion.7), channel_id=1, source_target_pairs={{0,16},{4,20},{8,24},{12,28},{16,0},{20,4},{24,8},{28,12},{1,17},{... | collective-permute-start | bytes 1572872 | tf_op jit(solution)/shard_map/ppermute | solution.py:42
  336.1 22.1 %collective-permute-start.59 = (bf16[256,1024]{1,0:T(8,128)(2,1)}, bf16[256,1024]{1,0:T(8,128)(2,1)S(1)}, u32[]{:S(2)}, u32[]{:S(2)}) collective-permute-start(bf16[256,1024]{1,0:T(8,128)(2,1)} %convolution_convert_fusion.5), channel_id=1, source_target_pairs={{0,8},{4,12},{8,0},{12,4},{16,24},{20,28},{24,16},{28,20},{1,9},{5... | collective-permute-start | bytes 1572872 | tf_op jit(solution)/shard_map/ppermute | solution.py:42
  349.2 112.1 %reduce-scatter.7.cloned.1.call-start = ((), (), s32[]{:S(2)}) async-start(), calls=%async_computation.9 | async-start | bytes 1310720 | tf_op jit(solution)/shard_map/reduce_scatter | solution.py:147
  355.1 19.7 %collective-permute-start.58 = (bf16[64,2048]{1,0:T(8,128)(2,1)S(1)}, bf16[64,2048]{1,0:T(8,128)(2,1)S(1)}, u32[]{:S(2)}, u32[]{:S(2)}) collective-permute-start(bf16[64,2048]{1,0:T(8,128)(2,1)S(1)} %collective-permute-done.57), channel_id=1, source_target_pairs={{0,1},{1,0},{2,3},{3,2},{4,5},{5,4},{6,7},{7,6},{8,9},{9,8},{10,11... | collective-permute-start | bytes 786440 | tf_op jit(solution)/shard_map/ppermute | solution.py:45
  357.3 41.2 %collective-permute-start.55 = (bf16[256,1024]{1,0:T(8,128)(2,1)S(1)}, bf16[256,1024]{1,0:T(8,128)(2,1)S(1)}, u32[]{:S(2)}, u32[]{:S(2)}) collective-permute-start(bf16[256,1024]{1,0:T(8,128)(2,1)S(1)} %add_convert_fusion.8), channel_id=1, source_target_pairs={{0,16},{4,20},{8,24},{12,28},{16,0},{20,4},{24,8},{28,12},{1,17},{... | collective-permute-start | bytes 1572872 | tf_op jit(solution)/shard_map/ppermute | solution.py:42
  359.5 50.4 %collective-permute-start.62 = (bf16[256,1024]{1,0:T(8,128)(2,1)S(1)}, bf16[256,1024]{1,0:T(8,128)(2,1)}, u32[]{:S(2)}, u32[]{:S(2)}) collective-permute-start(bf16[256,1024]{1,0:T(8,128)(2,1)S(1)} %add_convert_fusion.7), channel_id=1, source_target_pairs={{0,8},{4,12},{8,0},{12,4},{16,24},{20,28},{24,16},{28,20},{1,9},{5... | collective-permute-start | bytes 1572872 | tf_op jit(solution)/shard_map/ppermute | solution.py:42
  379.4 35.5 %collective-permute-start.66 = (bf16[256,1024]{1,0:T(8,128)(2,1)}, bf16[256,1024]{1,0:T(8,128)(2,1)}, u32[]{:S(2)}, u32[]{:S(2)}) collective-permute-start(bf16[256,1024]{1,0:T(8,128)(2,1)} %convolution_convert_fusion.3), channel_id=1, source_target_pairs={{0,16},{4,20},{8,24},{12,28},{16,0},{20,4},{24,8},{28,12},{1,17},{... | collective-permute-start | bytes 1572872 | tf_op jit(solution)/shard_map/ppermute | solution.py:42
  379.4 35.5 %collective-permute-start.65 = (bf16[256,1024]{1,0:T(8,128)(2,1)}, bf16[256,1024]{1,0:T(8,128)(2,1)}, u32[]{:S(2)}, u32[]{:S(2)}) collective-permute-start(bf16[256,1024]{1,0:T(8,128)(2,1)} %convolution_convert_fusion.1), channel_id=1, source_target_pairs={{0,8},{4,12},{8,0},{12,4},{16,24},{20,28},{24,16},{28,20},{1,9},{5... | collective-permute-start | bytes 1572872 | tf_op jit(solution)/shard_map/ppermute | solution.py:42
  416.3 18.5 %collective-permute-start.68 = (bf16[256,1024]{1,0:T(8,128)(2,1)S(1)}, bf16[256,1024]{1,0:T(8,128)(2,1)}, u32[]{:S(2)}, u32[]{:S(2)}) collective-permute-start(bf16[256,1024]{1,0:T(8,128)(2,1)S(1)} %add_convert_fusion.3), channel_id=1, source_target_pairs={{0,8},{4,12},{8,0},{12,4},{16,24},{20,28},{24,16},{28,20},{1,9},{5... | collective-permute-start | bytes 1572872 | tf_op jit(solution)/shard_map/ppermute | solution.py:42
  418.6 56.4 %reduce-scatter.9.cloned.1.call-start = ((), (), s32[]{:S(2)}) async-start(), calls=%async_computation.10 | async-start | bytes 1310720 | tf_op jit(solution)/shard_map/reduce_scatter | solution.py:147
  439.3 64.4 %reduce-scatter.11.cloned.1.call-start = ((), (), s32[]{:S(2)}) async-start(), calls=%async_computation.11 | async-start | bytes 1310720 | tf_op jit(solution)/shard_map/reduce_scatter | solution.py:147
  (101 other events, 916.9 us)
Sparse Core Ops, SparseCore 0:
  16.2 30.5 all-gather.4
  48.4 27.3 all-gather.6
  77.4 27.3 all-gather.8
  106.2 27.3 all-gather.10
  349.3 29.2 reduce-scatter.4
  418.7 28.1 reduce-scatter.6
  449.2 25.7 reduce-scatter.8
  477.9 25.7 reduce-scatter.10
